TPU v7x, 512 devices: a whole 4x8x8 slice. The times are simulated.
512 devices in a mesh: dp: 64 (over y, z), mp: 8 (over x, core).
Axes of the slice: x: 4, y: 8, z: 8, core: 2. Of those that a mesh axis runs over, the one named last changes fastest.
Arguments:
- inputs: bfloat16 [64, 2, 256, 2048], P('dp'), may hold values from -6 to 6
- grad_out: bfloat16 [64, 2, 256, 1024], P('dp', None, None, 'mp'), parts along dimension 3, may hold values from -0.5 to 0.5
- momentum: float32 [64, 2048, 1024], P('dp', None, 'mp'), parts along dimension 2, may hold values from -6 to 6
- select: int32 [64, 2, 64, 64], P(None, None, None, 'mp'), parts along dimension 3, may hold values from -1 to 31, as said below
Outputs:
- update: bfloat16 [2048, 1024], P(None, 'mp'), parts along dimension 1
- new_momentum: float32 [64, 2048, 1024], P('dp', None, 'mp'), parts along dimension 2
There are 8 independent parts, one for each index of `mp`. A program takes and returns all parts, laid end to end along the dimension named above; an argument that names none is the same for every part. Nothing has to cross between parts.
Inputs may be any that keep to these rules, and one draw needn't show every extreme that they name: `select`: in each [r, s, o] list the entries that are not -1 are distinct and come first. In every step some owner gets exactly 8 rows from every replica.
All inputs are finite; a program needn't handle non-finite values.
Results may differ from a plain program's by a relative error of at most 0.001.
Values sent between devices are 32-bit elements; how exact they have to be, the bound alone decides.
A program may use at most 64 MiB of HBM per device.

v0:
```python
import jax
import jax.numpy as jnp
from jax import lax
from jax.sharding import PartitionSpec as P

GROUP = 64


def from_everyone(array, axis):
    peers = lax.axis_size(axis)
    return lax.all_to_all(
        jnp.broadcast_to(array[None], (peers, *array.shape)), axis, 0, 0, tiled=True
    )


def in_order(parts, dim):
    parts = jnp.moveaxis(parts, 0, dim)
    dims = parts.shape
    return parts.reshape(*dims[:dim], dims[dim] * dims[dim + 1], *dims[dim + 2 :])


def gathered_copies(array, axis, dim):
    parts = from_everyone(array, axis)
    return in_order(parts, dim)


def dct_matrix(order):
    freq = lax.broadcasted_iota(jnp.int32, (order, order), 0).astype(jnp.float32)
    place = lax.broadcasted_iota(jnp.int32, (order, order), 1).astype(jnp.float32)
    factor = jnp.where(freq == 0.0, jnp.sqrt(1.0 / order), jnp.sqrt(2.0 / order)).astype(
        jnp.float32
    )
    return factor * jnp.cos(jnp.pi * (2.0 * place + 1.0) * freq / (2.0 * order))


def forward_blocks(field, dct_table, col_table):
    row_count, col_count = field.shape
    order = dct_table.shape[0]
    shaped = field.reshape(row_count // order, order, col_count)
    rowwise = jnp.einsum("ui,aic->auc", dct_table, shaped, precision=lax.Precision.HIGHEST)
    return jnp.dot(
        rowwise.reshape(row_count, col_count), col_table.T, precision=lax.Precision.HIGHEST
    )


def inverse_blocks(coeffs, dct_table, col_table):
    row_count, col_count = coeffs.shape
    order = dct_table.shape[0]
    colwise = jnp.dot(coeffs, col_table, precision=lax.Precision.HIGHEST)
    shaped = colwise.reshape(row_count // order, order, col_count)
    back = jnp.einsum("ui,auc->aic", dct_table, shaped, precision=lax.Precision.HIGHEST)
    return back.reshape(row_count, col_count)


def layer_gradient(inputs, grad_out, iteration):
    return lax.dot_general(
        inputs[0, iteration],
        grad_out[0, iteration],
        (((0,), (0,)), ((), ())),
        preferred_element_type=jnp.float32,
    )


def per_device(inputs, grad_out, momentum, select):
    replica = lax.axis_index("dp")
    owners = lax.axis_size("dp")
    step_count = inputs.shape[1]
    moment_state = momentum[0]
    row_count, col_count = moment_state.shape
    per_owner = row_count // owners
    slot_count = select.shape[3]
    dct_table = dct_matrix(GROUP)
    col_table = jnp.kron(jnp.eye(col_count // GROUP, dtype=jnp.float32), dct_table)
    own_select = lax.dynamic_index_in_dim(select, replica, 0, keepdims=False)
    owner_base = lax.broadcasted_iota(jnp.int32, (owners, slot_count), 0) * per_owner
    row_ids = lax.broadcasted_iota(jnp.int32, (1, row_count), 1)
    owned_ids = lax.broadcasted_iota(jnp.int32, (1, per_owner), 1)
    update_sum = jnp.zeros((row_count, col_count), jnp.float32)
    for iteration in range(step_count):
        gradient = layer_gradient(inputs, grad_out, iteration)
        moment_state = 0.999 * moment_state + gradient
        coefficients = forward_blocks(moment_state, dct_table, col_table)
        listed = own_select[iteration]
        usable = listed >= 0
        global_rows = jnp.where(usable, listed + owner_base, -1)
        chosen = jnp.any(global_rows.reshape(-1, 1) == row_ids, axis=0)
        sent = jnp.where(chosen[:, None], coefficients, 0.0)
        picked = coefficients[jnp.where(usable, global_rows, 0)]
        picked = jnp.where(usable[:, :, None], picked, 0.0)
        arrived = lax.all_to_all(picked, "dp", split_axis=0, concat_axis=0, tiled=True)
        local_rows = lax.dynamic_index_in_dim(select[:, iteration], replica, 1, keepdims=False)
        onehot = (local_rows.reshape(-1, 1) == owned_ids).astype(jnp.float32)
        owned_sums = lax.dot_general(
            onehot,
            arrived.reshape(-1, col_count),
            (((0,), (0,)), ((), ())),
            precision=lax.Precision.HIGHEST,
        )
        summed = gathered_copies(owned_sums, "dp", 0)
        update_sum = update_sum + inverse_blocks(summed, dct_table, col_table)
        moment_state = moment_state - inverse_blocks(sent, dct_table, col_table)
    return (update_sum.astype(jnp.bfloat16), moment_state[None])


def solution(mesh):
    return jax.shard_map(
        per_device,
        mesh=mesh,
        in_specs=(
            P("dp", None, None, None),
            P("dp", None, None, "mp"),
            P("dp", None, "mp"),
            P(None, None, None, "mp"),
        ),
        out_specs=(P(None, "mp"), P("dp", None, "mp")),
        check_vma=False,
    )
```

profile of v0, /device:TPU:6, one launch (start us, length us, event | category | flops | bytes accessed | tf_op | source)
XLA Modules:
  0.0 146.2 jit_solution(16792208848558467518)
XLA Ops:
  0.7 0.0 copy-start.3
  0.7 0.0 copy-start.5
  0.7 0.2 cosine_multiply_fusion
  0.9 0.1 copy.22
  1.0 0.1 broadcast_multiply_fusion
  1.1 0.1 mul.265
  1.2 0.1 reshape.319
  1.3 1.2 compare_bitcast_fusion
  2.6 0.1 copy.25
  2.7 0.1 squeeze.33
  2.8 0.1 copy.28
  2.9 0.1 squeeze.37
  2.9 0.6 compare_select_fusion
  3.6 0.1 iota.149
  3.6 0.1 iota.150
  3.7 2.1 %convolution_add_fusion.1 = f32[2048,128]{1,0:T(8,128)S(1)} fusion(bf16[1,2,256,2048]{3,2,1,0:T(8,128)(2,1)} %param.4, f32[1,2048,128]{2,1,0:T(8,128)} %param.6, bf16[1,2,256,128]{3,2,1,0:T(8,128)(2,1)} %param.5), kind=kOutput, calls=%fused_computation.7 | convolution fusion | flops 134742016 | bytes 3211264 | tf_op jit(solution)/shard_map/dot_general | solution.py:56
  5.8 1.2 fusion.27
  7.0 1.7 %fusion = (pred[2048]{0:T(1024)(128)(4,1)S(1)}, pred[2048]{0:T(1024)(128)(4,1)S(1)}) fusion(s32[512]{0:T(512)S(1)} %get-tuple-element.11, s32[512]{0:T(512)S(1)} %get-tuple-element.10), kind=kLoop, calls=%fused_computation.4 | loop fusion | flops 4190208 | bytes 8192 | tf_op jit(solution)/shard_map/reduce_or | solution.py:86
  8.7 1.0 broadcast_select_fusion.1
  9.7 1.0 fusion.61
  10.7 1.3 fusion.23
  12.0 0.0 copy-start
  12.0 0.0 copy-start.2
  12.0 0.1 fusion.3
  12.1 1.4 copy-done
  13.5 0.0 copy-done.2
  13.6 0.5 convolution_add_fusion
  14.1 2.2 %fusion.18 = f32[32,128,64]{1,2,0:T(8,128)} fusion(f32[32,64,128]{2,1,0:T(8,128)S(1)} %bitcast.109, f32[64]{0:T(128)S(1)} %convert_multiply_fusion, f32[64]{0:T(128)S(1)} %get-tuple-element.21, f32[64]{0:T(128)S(1)} %get-tuple-element.20), kind=kOutput, calls=%fused_computation.36 | convolution fusion | flops 201338880 | bytes 2097920 | tf_op jit(solution)/shard_map/ui,aic->auc/dot_general | solution.py:40
  16.3 0.1 copy.27
  16.3 0.1 reshape.310
  16.4 0.1 copy.24
  16.6 3.2 %broadcast_select_fusion = (f32[2048,128]{1,0:T(8,128)}, f32[2048,128]{1,0:T(8,128)S(1)}) fusion(pred[2048]{0:T(1024)(128)(4,1)S(1)} %get-tuple-element.19, f32[2048,128]{1,0:T(8,128)} %bitcast.115, f32[128,128]{1,0:T(8,128)S(1)} %mul.265), kind=kOutput, calls=%fused_computation.17 | convolution fusion | flops 402915328 | bytes 3213312 | tf_op jit(solution)/shard_map/dot_general | solution.py:41
  19.8 1.0 gather_fusion.1
  20.8 0.8 bitcast_select_fusion
  21.6 16.7 %all-to-all-start.2 = ((f32[64,8,128]{2,1,0:T(8,128)}), f32[64,8,128]{2,1,0:T(8,128)S(1)}, u32[]{:S(2)}, u32[]{:S(2)}) async-start(f32[64,8,128]{2,1,0:T(8,128)} %bitcast_select_fusion), calls=%async_computation.2 | async-start | bytes 524288 | tf_op jit(solution)/shard_map/all_to_all | solution.py:90
  38.4 0.0 copy-done.7
  38.4 0.1 copy.23
  38.5 0.1 reshape.302
  38.6 0.1 copy.20
  38.7 1.0 gather_fusion
  39.7 0.8 bitcast_select_fusion.1
  40.6 12.7 %all-to-all-done.2 = f32[64,8,128]{2,1,0:T(8,128)S(1)} async-done(((f32[64,8,128]{2,1,0:T(8,128)}), f32[64,8,128]{2,1,0:T(8,128)S(1)}, u32[]{:S(2)}, u32[]{:S(2)}) %all-to-all-start.2) | async-done | bytes 262176 | tf_op jit(solution)/shard_map/all_to_all | solution.py:90
  53.3 4.8 %all-to-all-start = ((f32[64,8,128]{2,1,0:T(8,128)}), f32[64,8,128]{2,1,0:T(8,128)S(1)}, u32[]{:S(2)}, u32[]{:S(2)}) async-start(f32[64,8,128]{2,1,0:T(8,128)} %bitcast_select_fusion.1), calls=%async_computation | async-start | bytes 524288 | tf_op jit(solution)/shard_map/all_to_all | solution.py:90
  58.1 0.0 copy-done.1
  58.2 1.2 dynamic-slice_reduce_fusion
  59.4 0.1 eq.109
  59.5 0.5 fusion.8
  60.0 12.2 %all-to-all-done = f32[64,8,128]{2,1,0:T(8,128)S(1)} async-done(((f32[64,8,128]{2,1,0:T(8,128)}), f32[64,8,128]{2,1,0:T(8,128)S(1)}, u32[]{:S(2)}, u32[]{:S(2)}) %all-to-all-start) | async-done | bytes 262176 | tf_op jit(solution)/shard_map/all_to_all | solution.py:90
  72.2 1.1 broadcast_in_dim.88
  73.2 4.7 %all-to-all-start.3 = ((f32[64,32,128]{2,1,0:T(8,128)}), f32[64,32,128]{2,1,0:T(8,128)S(1)}, u32[]{:S(2)}, u32[]{:S(2)}) async-start(f32[64,32,128]{2,1,0:T(8,128)} %broadcast_in_dim.88), calls=%async_computation.3 | async-start | bytes 2097152 | tf_op jit(solution)/shard_map/all_to_all | solution.py:11
  77.9 1.2 dynamic-slice_reduce_fusion.1
  79.2 0.1 eq.102
  79.3 0.5 fusion.10
  79.7 25.5 %all-to-all-done.3 = f32[64,32,128]{2,1,0:T(8,128)S(1)} async-done(((f32[64,32,128]{2,1,0:T(8,128)}), f32[64,32,128]{2,1,0:T(8,128)S(1)}, u32[]{:S(2)}, u32[]{:S(2)}) %all-to-all-start.3) | async-done | bytes 1048608 | tf_op jit(solution)/shard_map/all_to_all | solution.py:11
  105.2 1.1 broadcast_in_dim.83
  106.4 6.8 %all-to-all-start.1 = ((f32[64,32,128]{2,1,0:T(8,128)}), f32[64,32,128]{2,1,0:T(8,128)S(1)}, u32[]{:S(2)}, u32[]{:S(2)}) async-start(f32[64,32,128]{2,1,0:T(8,128)} %broadcast_in_dim.83), calls=%async_computation.1 | async-start | bytes 2097152 | tf_op jit(solution)/shard_map/all_to_all | solution.py:11
  113.2 2.2 %fusion.63 = f32[32,64,128]{2,1,0:T(8,128)S(1)} fusion(f32[32,64,128]{2,1,0:T(8,128)} %bitcast.113, f32[128,128,1]{1,0,2:T(8,128)S(1)} %reshape.319), kind=kOutput, calls=%fused_computation.103 | convolution fusion | flops 402653184 | bytes 2162688 | tf_op jit(solution)/shard_map/dot_general | solution.py:49
  115.4 1.3 fusion.20
  116.7 1.1 bitcast_subtract_fusion
  117.8 1.0 fusion.62
  118.7 23.1 %all-to-all-done.1 = f32[64,32,128]{2,1,0:T(8,128)S(1)} async-done(((f32[64,32,128]{2,1,0:T(8,128)}), f32[64,32,128]{2,1,0:T(8,128)S(1)}, u32[]{:S(2)}, u32[]{:S(2)}) %all-to-all-start.1) | async-done | bytes 1048608 | tf_op jit(solution)/shard_map/all_to_all | solution.py:11
  141.8 1.0 fusion.60
  142.8 1.3 fusion.25
  144.1 2.1 %fusion.2 = bf16[32,128,64]{1,2,0:T(8,128)(2,1)} fusion(f32[32,128,64]{1,2,0:T(8,128)S(1)} %fusion.25, f32[32,64,128]{2,1,0:T(8,128)S(1)} %fusion.62, f32[64]{0:T(128)S(1)} %copy-done.6, f32[64]{0:T(128)S(1)} %copy-done.4, f32[64]{0:T(128)S(1)} %get-tuple-element.20), kind=kOutput, calls=%fused_computation.9 | convolution fusion | flops 201863168 | bytes 2622208 | tf_op jit(solution)/shard_map/ui,auc->aic/dot_general | solution.py:51
  (18 shorter events, 0.1 us)
Async XLA Ops:
  0.7 13.4 %copy-start.3 = (f32[64]{0:T(128)}, f32[64]{0:T(128)S(1)}, u32[]{:S(2)}) copy-start(f32[64]{0:T(128)S(1)} %get-tuple-element.21) | copy-start | bytes 772
  0.7 13.4 %copy-start.5 = (f32[64]{0:T(128)}, f32[64]{0:T(128)S(1)}, u32[]{:S(2)}) copy-start(f32[64]{0:T(128)S(1)} %convert_multiply_fusion) | copy-start | bytes 772
  12.0 1.6 %copy-start = (bf16[1,2,256,2048]{3,2,1,0:T(8,128)(2,1)S(1)}, bf16[1,2,256,2048]{3,2,1,0:T(8,128)(2,1)}, u32[]{:S(2)}) copy-start(bf16[1,2,256,2048]{3,2,1,0:T(8,128)(2,1)} %param.4) | copy-start | bytes 6291460
  12.0 1.6 %copy-start.2 = (bf16[1,2,256,128]{3,2,1,0:T(8,128)(2,1)S(1)}, bf16[1,2,256,128]{3,2,1,0:T(8,128)(2,1)}, u32[]{:S(2)}) copy-start(bf16[1,2,256,128]{3,2,1,0:T(8,128)(2,1)} %param.5) | copy-start | bytes 393220
  19.8 18.6 %copy-start.7 = (s32[64,8,1]{0,1,2:T(8,128)S(1)}, s32[64,8,1]{0,1,2:T(8,128)}, u32[]{:S(2)}) copy-start(s32[64,8,1]{0,1,2:T(8,128)} %get-tuple-element.13) | copy-start | bytes 6148
  19.8 18.8 %copy-start.8 = (pred[64,8]{0,1:T(8,128)(4,1)S(1)}, pred[64,8]{0,1:T(8,128)(4,1)}, u32[]{:S(2)}) copy-start(pred[64,8]{0,1:T(8,128)(4,1)} %get-tuple-element.8) | copy-start | bytes 1540
  21.6 36.5 %copy-start.1 = (s32[64,2,64,8]{2,3,1,0:T(8,128)S(1)}, s32[64,2,64,8]{2,3,1,0:T(8,128)}, u32[]{:S(2)}) copy-start(s32[64,2,64,8]{2,3,1,0:T(8,128)} %param.7) | copy-start | bytes 786436
  21.6 31.7 %all-to-all-start.2 = ((f32[64,8,128]{2,1,0:T(8,128)}), f32[64,8,128]{2,1,0:T(8,128)S(1)}, u32[]{:S(2)}, u32[]{:S(2)}) async-start(f32[64,8,128]{2,1,0:T(8,128)} %bitcast_select_fusion), calls=%async_computation.2 | async-start | bytes 524288 | tf_op jit(solution)/shard_map/all_to_all | solution.py:90
  53.3 18.8 %all-to-all-start = ((f32[64,8,128]{2,1,0:T(8,128)}), f32[64,8,128]{2,1,0:T(8,128)S(1)}, u32[]{:S(2)}, u32[]{:S(2)}) async-start(f32[64,8,128]{2,1,0:T(8,128)} %bitcast_select_fusion.1), calls=%async_computation | async-start | bytes 524288 | tf_op jit(solution)/shard_map/all_to_all | solution.py:90
  73.2 32.0 %all-to-all-start.3 = ((f32[64,32,128]{2,1,0:T(8,128)}), f32[64,32,128]{2,1,0:T(8,128)S(1)}, u32[]{:S(2)}, u32[]{:S(2)}) async-start(f32[64,32,128]{2,1,0:T(8,128)} %broadcast_in_dim.88), calls=%async_computation.3 | async-start | bytes 2097152 | tf_op jit(solution)/shard_map/all_to_all | solution.py:11
  106.3 9.0 %copy-start.4 = (f32[64]{0:T(128)S(1)}, f32[64]{0:T(128)}, u32[]{:S(2)}) copy-start(f32[64]{0:T(128)} %copy-done.3) | copy-start | bytes 772
  106.4 9.0 %copy-start.6 = (f32[64]{0:T(128)S(1)}, f32[64]{0:T(128)}, u32[]{:S(2)}) copy-start(f32[64]{0:T(128)} %copy-done.5) | copy-start | bytes 772
  106.4 35.5 %all-to-all-start.1 = ((f32[64,32,128]{2,1,0:T(8,128)}), f32[64,32,128]{2,1,0:T(8,128)S(1)}, u32[]{:S(2)}, u32[]{:S(2)}) async-start(f32[64,32,128]{2,1,0:T(8,128)} %broadcast_in_dim.83), calls=%async_computation.1 | async-start | bytes 2097152 | tf_op jit(solution)/shard_map/all_to_all | solution.py:11
where the time goes:
time: 147 us; the launch traced here: 146 us
  waiting for transfers between devices  73.5 us (50%)
  starting transfers between devices  33 us (22%)
  matrix products  22.1 us (15%)
  local copies, waits for them, and re-layouts  9.86 us (7%)
  other arithmetic  6.72 us (5%)
    all_to_all x2, waiting for transfers between devices, from_everyone(): lax.all_to_all(jnp.broadcast_to(array[None], (peers, *array.shape)), axis...  48.6 us
    all_to_all x2, waiting for transfers between devices, per_device(): lax.all_to_all(picked, 'dp', split_axis=0, concat_axis=0, tiled=True)  24.9 us
    all_to_all x2, starting transfers between devices, per_device(): lax.all_to_all(picked, 'dp', split_axis=0, concat_axis=0, tiled=True)  21.5 us
    all_to_all x2, starting transfers between devices, from_everyone(): lax.all_to_all(jnp.broadcast_to(array[None], (peers, *array.shape)), axis...  11.5 us
    dot_general x4, matrix products, inverse_blocks(): jnp.einsum('ui,auc->aic', dct_table, shaped, precision=lax.Precision.HIGH...  5.96 us
    dot_general x4, matrix products, inverse_blocks(): colwise = jnp.dot(coeffs, col_table, precision=lax.Precision.HIGHEST)  5.09 us
    dot_general x2, matrix products, forward_blocks(): jnp.dot(rowwise.reshape(row_count, col_count), col_table.T, precision=lax...  4.2 us
    dot_general x2, matrix products, forward_blocks(): jnp.einsum('ui,aic->auc', dct_table, shaped, precision=lax.Precision.HIGH...  3.4 us
  transfers between devices with their start and end apart: 4, of which 4 were waited for; matrix products, arithmetic and copies ran while one was open for 8% of the time, Pallas kernels for 0%

commit v1 on v0

v1 whole, which is shorter than its diff:
```python
import jax
import jax.numpy as jnp
from jax import lax
from jax.sharding import PartitionSpec as P

GROUP = 64
DECAY = 0.999


def dct_matrix(order):
    freq = lax.broadcasted_iota(jnp.int32, (order, order), 0).astype(jnp.float32)
    place = lax.broadcasted_iota(jnp.int32, (order, order), 1).astype(jnp.float32)
    factor = jnp.where(freq == 0.0, jnp.sqrt(1.0 / order), jnp.sqrt(2.0 / order)).astype(
        jnp.float32
    )
    return factor * jnp.cos(jnp.pi * (2.0 * place + 1.0) * freq / (2.0 * order))


def forward_blocks(field, dct_table, col_table):
    row_count, col_count = field.shape
    order = dct_table.shape[0]
    shaped = field.reshape(row_count // order, order, col_count)
    rowwise = jnp.einsum("ui,aic->auc", dct_table, shaped, precision=lax.Precision.HIGHEST)
    return jnp.dot(
        rowwise.reshape(row_count, col_count), col_table.T, precision=lax.Precision.HIGHEST
    )


def inverse_blocks(coeffs, dct_table, col_table):
    row_count, col_count = coeffs.shape
    order = dct_table.shape[0]
    colwise = jnp.dot(coeffs, col_table, precision=lax.Precision.HIGHEST)
    shaped = colwise.reshape(row_count // order, order, col_count)
    back = jnp.einsum("ui,auc->aic", dct_table, shaped, precision=lax.Precision.HIGHEST)
    return back.reshape(row_count, col_count)


def layer_gradient(inputs, grad_out, iteration):
    return lax.dot_general(
        inputs[0, iteration],
        grad_out[0, iteration],
        (((0,), (0,)), ((), ())),
        preferred_element_type=jnp.float32,
    )


def per_device(inputs, grad_out, momentum, select):
    replica = lax.axis_index("dp")
    owners = lax.axis_size("dp")
    row_count, col_count = momentum.shape[1:]
    per_owner = row_count // owners
    dct_table = dct_matrix(GROUP)
    col_table = jnp.kron(jnp.eye(col_count // GROUP, dtype=jnp.float32), dct_table)
    own_select = lax.dynamic_index_in_dim(select, replica, 0, keepdims=False)
    row_ids = lax.broadcasted_iota(jnp.int32, (1, per_owner, 1), 1)
    kept = None
    sent_total = 0.0
    field = DECAY * momentum[0] + layer_gradient(inputs, grad_out, 0)
    for iteration in range(inputs.shape[1]):
        if iteration:
            field = layer_gradient(inputs, grad_out, iteration)
        coefficients = forward_blocks(field, dct_table, col_table)
        if iteration:
            coefficients = coefficients + DECAY * kept
        listed = own_select[iteration]
        chosen = jnp.any(listed[:, None, :] == row_ids, axis=2)
        chosen = chosen.reshape(row_count, 1)
        sent_total = sent_total + jnp.where(chosen, coefficients, 0.0)
        kept = jnp.where(chosen, 0.0, coefficients)
    summed = lax.psum(sent_total, "dp")
    update = inverse_blocks(summed, dct_table, col_table)
    new_momentum = inverse_blocks(kept, dct_table, col_table)
    return (update.astype(jnp.bfloat16), new_momentum[None])


def solution(mesh):
    return jax.shard_map(
        per_device,
        mesh=mesh,
        in_specs=(
            P("dp", None, None, None),
            P("dp", None, None, "mp"),
            P("dp", None, "mp"),
            P(None, None, None, "mp"),
        ),
        out_specs=(P(None, "mp"), P("dp", None, "mp")),
        check_vma=False,
    )
```

time: 147 us -> 195 us (1.33)
  waiting for transfers between devices: 73.5 us -> 163 us
  starting transfers between devices: 33 us -> 0.04 us
  between operations: 0.95 us -> 14.2 us
  local copies, waits for them, and re-layouts: 9.86 us -> 2.1 us
  matrix products: 22.1 us -> 15.8 us
  other arithmetic: 6.72 us -> 0.43 us
    psum x0 -> x1, waiting for transfers between devices: none -> 163 us  [per_device(): summed = lax.psum(sent_total, 'dp')]
    all_to_all x4 -> x0, waiting for transfers between devices: 73.5 us -> none  [the longest x2 48.6 us: from_everyone(): lax.all_to_all(jnp.broadcast_to(array[None], (peers, *array.shape)), axis...]
    all_to_all x4 -> x0, starting transfers between devices: 33 us -> none  [the longest x2 21.5 us: per_device(): lax.all_to_all(picked, 'dp', split_axis=0, concat_axis=0, tiled=True)]
    dynamic_slice x2 -> x0, local copies, waits for them, and re-layouts: 2.49 us -> none  [per_device(): lax.dynamic_index_in_dim(select[:, iteration], replica, 1, keepdims=False)]
    select_n x4 -> x0, other arithmetic: 2.29 us -> none  [the longest x2 1.68 us: per_device(): picked = jnp.where(usable[:, :, None], picked, 0.0)]
    gather x2 -> x0, local copies, waits for them, and re-layouts: 2.06 us -> none  [per_device(): picked = coefficients[jnp.where(usable, global_rows, 0)]]
    broadcast_in_dim x2, local copies, waits for them, and re-layouts: 2.2 us -> 0.18 us  [per_device(): sent_total = sent_total + jnp.where(chosen, coefficients, 0.0)]
    dot_general x4 -> x2, matrix products: 5.09 us -> 3.15 us  [inverse_blocks(): colwise = jnp.dot(coeffs, col_table, precision=lax.Precision.HIGHEST)]
  transfers between devices with their start and end apart: 4 -> 1, of which waited for: 4 -> 1; matrix products, arithmetic and copies ran while one was open for 8% -> 2% of each run, Pallas kernels for 0% -> 0%
where the time goes in v1:
time: 195 us
  waiting for transfers between devices  163 us (84%)
  matrix products  15.8 us (8%)
  between operations  14.2 us (7%)
  local copies, waits for them, and re-layouts  2.1 us (1%)
    psum x1, waiting for transfers between devices, per_device(): summed = lax.psum(sent_total, 'dp')  163 us
    dot_general x2, matrix products, inverse_blocks(): jnp.einsum('ui,auc->aic', dct_table, shaped, precision=lax.Precision.HIGH...  4.33 us
  transfers between devices with their start and end apart: 1, of which 1 were waited for; matrix products, arithmetic and copies ran while one was open for 2% of the time, Pallas kernels for 0%

profile of v1, /device:TPU:6, one launch (start us, length us, event | category | flops | bytes accessed | tf_op | source)
XLA Modules:
  0.0 195.2 jit_solution(3792753614585185426)
XLA Ops:
  7.2 0.0 copy-start
  7.2 0.0 copy-start.1
  7.2 0.0 all-reduce.2.cloned.1.call-start
  7.3 0.8 dynamic-slice_bitcast_fusion
  8.1 0.1 fusion.2
  8.2 0.1 copy.17
  8.3 0.1 broadcast_in_dim.46
  8.4 0.1 copy.20
  8.5 0.1 broadcast_in_dim.51
  8.6 0.2 cosine_multiply_fusion
  8.8 0.1 copy.19
  8.9 0.1 broadcast_multiply_fusion
  9.0 0.1 mul.188
  9.1 0.0 copy-done
  9.1 0.0 copy-done.1
  9.1 1.7 convolution_add_fusion.1
  10.9 0.0 slice-start
  10.9 1.2 fusion.14
  12.1 0.0 slice-done
  12.1 0.5 copy.27
  12.6 0.4 fusion.4
  13.1 1.2 fusion.12
  14.3 1.0 fusion.36
  15.3 2.7 %broadcast_select_fusion = (f32[2048,128]{1,0:T(8,128)S(1)}, f32[2048,128]{1,0:T(8,128)}) fusion(pred[2048]{0:T(1024)(128)(4,1)S(1)} %broadcast_in_dim.51, f32[2048,128]{1,0:T(8,128)S(1)} %fusion.36, pred[2048]{0:T(1024)(128)(4,1)S(1)} %broadcast_in_dim.46, f32[2048,128]{1,0:T(8,128)S(1)} %bitcast.63, f32[128,128]{1,0:T(8,128)S(1)} %mul.188), kind=kOutput, calls=%fused_computation.6 | convolution fusion | flops 404488192 | bytes 4263936 | tf_op jit(solution)/shard_map/dot_general | solution.py:24
  18.0 0.0 all-reduce.2.cloned.1.call-update
  18.1 0.1 reshape.107
  18.2 1.0 fusion.38
  19.2 2.3 %fusion.9 = f32[32,128,64]{1,2,0:T(8,128)} fusion(f32[32,64,128]{2,1,0:T(8,128)S(1)} %fusion.38, f32[64]{0:T(128)S(1)} %convert_multiply_fusion, f32[64]{0:T(128)S(1)} %get-tuple-element.9, f32[64]{0:T(128)S(1)} %get-tuple-element.8), kind=kOutput, calls=%fused_computation.17 | convolution fusion | flops 201338880 | bytes 2097920 | tf_op jit(solution)/shard_map/ui,auc->aic/dot_general | solution.py:34
  21.4 162.6 %all-reduce.2.cloned.1.call-done = f32[32,64,128]{2,1,0:T(8,128)} async-done(((f32[32,64,128]{2,1,0:T(8,128)}), f32[32,64,128]{2,1,0:T(8,128)}) %all-reduce.2.cloned.1.call-update) | async-done | bytes 1048592 | tf_op jit(solution)/shard_map/psum | solution.py:70
  184.1 2.2 %fusion.37 = f32[32,64,128]{2,1,0:T(8,128)S(1)} fusion(f32[32,64,128]{2,1,0:T(8,128)} %all-reduce.2.cloned.1.call-done, f32[128,128,1]{1,0,2:T(8,128)S(1)} %reshape.107), kind=kOutput, calls=%fused_computation.52 | convolution fusion | flops 402653184 | bytes 2162688 | tf_op jit(solution)/shard_map/dot_general | solution.py:32
  186.3 2.1 %convolution_convert_fusion = bf16[32,128,64]{1,2,0:T(8,128)(2,1)} fusion(f32[32,64,128]{2,1,0:T(8,128)S(1)} %fusion.37, f32[64]{0:T(128)S(1)} %convert_multiply_fusion, f32[64]{0:T(128)S(1)} %get-tuple-element.9, f32[64]{0:T(128)S(1)} %get-tuple-element.8), kind=kOutput, calls=%fused_computation.2 | convolution fusion | flops 201601024 | bytes 1573632 | tf_op jit(solution)/shard_map/ui,auc->aic/dot_general | solution.py:34
  (3 shorter events, 0.0 us)
Async XLA Ops:
  7.2 2.0 %copy-start = (bf16[1,2,256,2048]{3,2,1,0:T(8,128)(2,1)S(1)}, bf16[1,2,256,2048]{3,2,1,0:T(8,128)(2,1)}, u32[]{:S(2)}) copy-start(bf16[1,2,256,2048]{3,2,1,0:T(8,128)(2,1)} %param.4) | copy-start | bytes 6291460
  7.2 2.0 %copy-start.1 = (bf16[1,2,256,128]{3,2,1,0:T(8,128)(2,1)S(1)}, bf16[1,2,256,128]{3,2,1,0:T(8,128)(2,1)}, u32[]{:S(2)}) copy-start(bf16[1,2,256,128]{3,2,1,0:T(8,128)(2,1)} %param.5) | copy-start | bytes 393220
  7.2 176.9 %all-reduce.2.cloned.1.call-start = ((), (), s32[]{:S(2)}) async-start(), calls=%async_computation | async-start | bytes 2097152 | tf_op jit(solution)/shard_map/psum | solution.py:70
  10.9 1.2 slice-start
Sparse Core Ops, SparseCore 0:
  18.2 165.8 all-reduce.1

commit v2 on v1

v2 whole, which is shorter than its diff:
```python
import jax
import jax.numpy as jnp
import numpy as np
from jax import lax
from jax.experimental import pallas as pl
from jax.experimental.pallas import tpu as pltpu
from jax.sharding import PartitionSpec as P

GROUP = 64
DECAY = 0.999
SIDE = 8
PER_OWNER = 32
CAP = 8
STEPS = 2
ROWS = 2048
COLS = 128
TOK = 256
SPAN = 256
BF16 = jnp.bfloat16
F32 = jnp.float32
MESH = pl.DeviceIdType.MESH
FAR_FIRST = (4, 3, 5, 2, 6, 1, 7)


def transform_tables():
    u = np.arange(GROUP)[:, None].astype(np.float64)
    i = np.arange(GROUP)[None, :].astype(np.float64)
    scale = np.where(u == 0, np.sqrt(1.0 / GROUP), np.sqrt(2.0 / GROUP))
    dct = (scale * np.cos(np.pi * (2 * i + 1) * u / (2 * GROUP))).astype(np.float32)
    rows = np.kron(np.eye(SPAN // GROUP, dtype=np.float32), dct)
    cols = np.kron(np.eye(COLS // GROUP, dtype=np.float32), dct)

    def halves(table):
        high = table.astype(BF16)
        low = (table - high.astype(np.float32)).astype(BF16)
        return high, low

    def by_column(table):
        high, low = halves(table)
        zero = np.zeros_like(low)
        return np.concatenate(
            [np.concatenate([high, low], 1), np.concatenate([high, zero], 1)], 0
        )

    def by_row(table):
        return np.concatenate(halves(table), 0)

    return np.concatenate(
        [by_column(cols.T), by_row(rows), by_column(cols), by_row(rows.T)], 0
    )


TABLE_ROWS = 1536


def split(x):
    high = x.astype(BF16)
    low = (x - high.astype(F32)).astype(BF16)
    return jnp.concatenate([high, low], axis=1)


def dot(a, b, dims=(((1,), (0,)), ((), ()))):
    return lax.dot_general(a, b, dims, preferred_element_type=F32)


def folded(x):
    return x[:, :COLS] + x[:, COLS:]


def row_apply(table, x):
    r = dot(table, split(x))
    return r[:SPAN, :COLS] + (r[:SPAN, COLS:] + r[SPAN:, :COLS])


def kernel(
    x_hbm, g_hbm, m_hbm, sel_hbm, tab_hbm,
    upd_ref, mom_ref,
    x_v, g_v, m_v, sel_v, tab_v, h_v, f_v, c_v, kept_v,
    zsend, ysend, zin, yin, pz, py, p2in, tout, u_v,
    load_sem, r1s, r1r, p2s, p2r, a1s, a1r, a2s, a2r,
):
    me = lax.axis_index("dp")
    mp = lax.axis_index("mp")
    y = me // SIDE
    z = me % SIDE
    par = (y + z) % 2

    def at(yy, zz):
        return (yy * SIDE + zz, mp)

    loads = []

    def load(src, dst):
        copy = pltpu.make_async_copy(src, dst, load_sem.at[len(loads)])
        copy.start()
        loads.append(copy)
        return copy

    load_g = load(g_hbm.at[0], g_v)
    load_tab = load(tab_hbm.at[pl.ds(0, 768)], tab_v.at[pl.ds(0, 768)])
    load_x0 = load(x_hbm.at[0, 0], x_v.at[0])
    load_m = load(m_hbm.at[0], m_v)
    load_sel = load(sel_hbm, sel_v)
    load_x1 = load(x_hbm.at[0, 1], x_v.at[1])
    load_tab2 = load(tab_hbm.at[pl.ds(768, 768)], tab_v.at[pl.ds(768, 768)])

    barrier = pltpu.get_barrier_semaphore()
    for d in range(1, SIDE):
        pl.semaphore_signal(barrier, inc=1, device_id=at((y + d) % SIDE, z), device_id_type=MESH)
        pl.semaphore_signal(barrier, inc=1, device_id=at(y, (z + d) % SIDE), device_id_type=MESH)

    load_g.wait()
    load_tab.wait()
    for s in range(STEPS):
        h_v[s] = split(folded(dot(g_v[s], tab_v[0:COLS, :])))

    tn = (((0,), (0,)), ((), ()))
    load_x0.wait()
    load_m.wait()
    for g in range(SIDE):
        rows = pl.ds(g * SPAN, SPAN)
        grad = folded(dot(x_v[0, :, rows], h_v[0], tn))
        carried = folded(dot(split(m_v[rows, :]), tab_v[0:SPAN, :]))
        f_v[0, g] = DECAY * carried + grad
    load_x1.wait()
    for g in range(SIDE):
        rows = pl.ds(g * SPAN, SPAN)
        f_v[1, g] = folded(dot(x_v[1, :, rows], h_v[1], tn))

    load_sel.wait()
    lane = lax.broadcasted_iota(jnp.int32, (CAP, SPAN), 1)
    ones = jnp.ones((SIDE * CAP, COLS), BF16)
    owner_lane = lax.broadcasted_iota(jnp.int32, (CAP, SIDE * SIDE), 1)
    forward = tab_v[256:768, :]
    for s in range(STEPS):
        own = sel_v[me, s]
        own = jnp.where(own >= 0, own + (owner_lane % SIDE) * PER_OWNER, -1)
        for g in range(SIDE):
            c = row_apply(forward, f_v[s, g])
            if s:
                c = c + DECAY * kept_v[g]
            picks = [
                (own[:, g * SIDE + q : g * SIDE + q + 1] == lane).astype(F32)
                for q in range(SIDE)
            ]
            onehot = jnp.concatenate(picks, axis=0).astype(BF16)
            mask = dot(onehot, ones, tn)
            packed = folded(dot(onehot, split(c)))
            kept_v[g] = jnp.where(mask > 0.5, 0.0, c)
            for q in range(SIDE):
                tile = packed[q * CAP : (q + 1) * CAP]
                if (g + q) % 2 == 0:
                    zsend[q, g // 2, s * CAP : (s + 1) * CAP, :] = tile
                else:
                    ysend[g, q // 2, s * CAP : (s + 1) * CAP, :] = tile

    pl.semaphore_wait(barrier, 2 * (SIDE - 1))

    def first(axis, d):
        if axis == 0:
            to = (z + d) % SIDE
            return pltpu.make_async_remote_copy(
                src_ref=zsend.at[to], dst_ref=zin.at[z],
                send_sem=r1s.at[0, d], recv_sem=r1r.at[0, d],
                device_id=at(y, to), device_id_type=MESH,
            )
        to = (y + d) % SIDE
        return pltpu.make_async_remote_copy(
            src_ref=ysend.at[to], dst_ref=yin.at[y],
            send_sem=r1s.at[1, d], recv_sem=r1r.at[1, d],
            device_id=at(to, z), device_id_type=MESH,
        )

    for d in FAR_FIRST:
        for axis in range(2):
            first(axis, d).start()
    zin[z] = zsend[z]
    yin[y] = ysend[y]

    load_tab2.wait()
    pick_row = lax.broadcasted_iota(jnp.int32, (COLS, SIDE * SIDE), 0)
    pick_lane = lax.broadcasted_iota(jnp.int32, (COLS, SIDE * SIDE), 1)
    place = (lax.broadcasted_iota(jnp.int32, (COLS, COLS), 0) % PER_OWNER).astype(F32)
    nt = (((1,), (1,)), ((), ()))

    def scatter_table(listed, owner):
        chooser = (pick_lane == owner).astype(F32).astype(BF16)
        wanted = dot(chooser, listed.astype(F32).astype(BF16), nt)
        return (wanted == place).astype(F32).astype(BF16)

    along_z = sel_v[pl.ds(y * SIDE, SIDE)].reshape(COLS, SIDE * SIDE)
    along_y = jnp.concatenate(
        [sel_v[q * SIDE + z].reshape(STEPS * CAP, SIDE * SIDE) for q in range(SIDE)], axis=0
    )
    index = pick_row // PER_OWNER
    table_z = scatter_table(along_z, (2 * index + z % 2) * SIDE + z)
    table_y = scatter_table(along_y, y * SIDE + 2 * index + (y + 1) % 2)

    by_col = tab_v[768:1024, :]
    backward = tab_v[1024:1536, :]
    for g in range(SIDE):
        f_v[0, g] = folded(dot(split(kept_v[g]), by_col))
    for g in range(SIDE):
        mom_ref[g * SPAN : (g + 1) * SPAN, :] = row_apply(backward, f_v[0, g])

    for d in FAR_FIRST:
        for axis in range(2):
            first(axis, d).wait_recv()
    for i in range(4):
        block = slice(i * PER_OWNER, (i + 1) * PER_OWNER)
        pz[i] = folded(dot(table_z[block], split(zin[:, i].reshape(COLS, COLS))))
        py[i] = folded(dot(table_y[block], split(yin[:, i].reshape(COLS, COLS))))

    def second(axis, i):
        if axis == 0:
            to = 2 * i + z % 2
            return to != y, pltpu.make_async_remote_copy(
                src_ref=pz.at[i], dst_ref=p2in.at[y],
                send_sem=p2s.at[0, i], recv_sem=p2r.at[y],
                device_id=at(to, z), device_id_type=MESH,
            )
        to = 2 * i + (y + 1) % 2
        return to != z, pltpu.make_async_remote_copy(
            src_ref=py.at[i], dst_ref=p2in.at[z],
            send_sem=p2s.at[1, i], recv_sem=p2r.at[z],
            device_id=at(y, to), device_id_type=MESH,
        )

    for i in range(4):
        for axis in range(2):
            other, copy = second(axis, i)

            @pl.when(other)
            def _():
                copy.start()

            @pl.when(jnp.logical_not(other))
            def _():
                if axis == 0:
                    p2in[y] = pz[i]
                else:
                    p2in[z] = py[i]

    slot = y + par * (z - y)
    for k in range(SIDE):

        @pl.when(k != slot)
        def _():
            pltpu.make_async_remote_copy(
                src_ref=pz.at[0], dst_ref=p2in.at[k],
                send_sem=p2s.at[0, 0], recv_sem=p2r.at[k],
                device_id=at((y + 1) % SIDE, z), device_id_type=MESH,
            ).wait_recv()

    total = p2in[0]
    for k in range(1, SIDE):
        total = total + p2in[k]
    line = z + par * (y - z)
    mine = (y + par * (z - y)) // 2
    final = folded(dot(split(total), by_col))
    tout[...] = final
    u_v[par, line, mine] = final

    def third(d):
        to_y = (y + (1 - par) * d) % SIDE
        to_z = (z + par * d) % SIDE
        return pltpu.make_async_remote_copy(
            src_ref=tout, dst_ref=u_v.at[par, line, mine],
            send_sem=a1s.at[d], recv_sem=a1r.at[par, mine],
            device_id=at(to_y, to_z), device_id_type=MESH,
        )

    for d in FAR_FIRST:
        third(d).start()

    def third_arrived(axis, i):
        where = z if axis == 0 else y
        own = (par == axis) & (mine == i)

        @pl.when(jnp.logical_not(own))
        def _():
            pltpu.make_async_remote_copy(
                src_ref=tout, dst_ref=u_v.at[axis, where, i],
                send_sem=a1s.at[1], recv_sem=a1r.at[axis, i],
                device_id=at((y + 1) % SIDE, z), device_id_type=MESH,
            ).wait_recv()

    def relay(axis, way, level, half):
        pos = z if axis == 0 else y
        step = 1 if way == 0 else SIDE - 1
        source = (pos + (level - 1) * (SIDE - step)) % SIDE
        to = (pos + step) % SIDE
        block = u_v.at[axis, source, pl.ds(half * 2, 2)]
        return pltpu.make_async_remote_copy(
            src_ref=block, dst_ref=block,
            send_sem=a2s.at[axis, way, level - 1, half],
            recv_sem=a2r.at[axis, way, level - 1, half],
            device_id=at(y, to) if axis == 0 else at(to, z), device_id_type=MESH,
        )

    def relay_arrived(axis, way, level, half):
        pos = z if axis == 0 else y
        step = 1 if way == 0 else SIDE - 1
        source = (pos + level * (SIDE - step)) % SIDE
        block = u_v.at[axis, source, pl.ds(half * 2, 2)]
        pltpu.make_async_remote_copy(
            src_ref=block, dst_ref=block,
            send_sem=a2s.at[axis, way, level - 1, half],
            recv_sem=a2r.at[axis, way, level - 1, half],
            device_id=at((y + 1) % SIDE, z), device_id_type=MESH,
        ).wait_recv()

    def levels(way, half):
        return 4 if way == half else 3

    sent = []
    for half in range(2):
        for axis in range(2):
            for i in (2 * half, 2 * half + 1):
                third_arrived(axis, i)
            for way in range(2):
                copy = relay(axis, way, 1, half)
                copy.start()
                sent.append(copy)
    for level in range(1, 5):
        for half in range(2):
            for axis in range(2):
                for way in range(2):
                    if level <= levels(way, half):
                        relay_arrived(axis, way, level, half)
                        if level < levels(way, half):
                            copy = relay(axis, way, level + 1, half)
                            copy.start()
                            sent.append(copy)

    for g in range(SIDE):
        parts = [
            u_v[0, q, g // 2] if (g + q) % 2 == 0 else u_v[1, g, q // 2] for q in range(SIDE)
        ]
        block = row_apply(backward, jnp.concatenate(parts, axis=0))
        upd_ref[g * SPAN : (g + 1) * SPAN, :] = block.astype(BF16)

    for d in FAR_FIRST:
        for axis in range(2):
            first(axis, d).wait_send()
    for i in range(4):
        for axis in range(2):
            other, copy = second(axis, i)

            @pl.when(other)
            def _():
                copy.wait_send()

    for d in FAR_FIRST:
        third(d).wait_send()
    for copy in sent:
        copy.wait_send()


def per_device(inputs, grad_out, momentum, select):
    table = jnp.asarray(transform_tables())
    listed = jnp.transpose(select, (0, 1, 3, 2))
    hbm = pl.BlockSpec(memory_space=pl.ANY)
    vmem = pl.BlockSpec(memory_space=pltpu.VMEM)
    update, new_momentum = pl.pallas_call(
        kernel,
        out_shape=(
            jax.ShapeDtypeStruct((ROWS, COLS), BF16),
            jax.ShapeDtypeStruct((ROWS, COLS), F32),
        ),
        in_specs=[hbm] * 5,
        out_specs=(vmem, vmem),
        scratch_shapes=[
            pltpu.VMEM((STEPS, TOK, ROWS), BF16),
            pltpu.VMEM((STEPS, TOK, COLS), BF16),
            pltpu.VMEM((ROWS, COLS), F32),
            pltpu.VMEM((SIDE * SIDE, STEPS, CAP, SIDE * SIDE), jnp.int32),
            pltpu.VMEM((TABLE_ROWS, SPAN), BF16),
            pltpu.VMEM((STEPS, TOK, 2 * COLS), BF16),
            pltpu.VMEM((STEPS, SIDE, SPAN, COLS), F32),
            pltpu.VMEM((8, COLS), F32),
            pltpu.VMEM((SIDE, SPAN, COLS), F32),
            pltpu.VMEM((SIDE, 4, STEPS * CAP, COLS), F32),
            pltpu.VMEM((SIDE, 4, STEPS * CAP, COLS), F32),
            pltpu.VMEM((SIDE, 4, STEPS * CAP, COLS), F32),
            pltpu.VMEM((SIDE, 4, STEPS * CAP, COLS), F32),
            pltpu.VMEM((4, PER_OWNER, COLS), F32),
            pltpu.VMEM((4, PER_OWNER, COLS), F32),
            pltpu.VMEM((SIDE, PER_OWNER, COLS), F32),
            pltpu.VMEM((PER_OWNER, COLS), F32),
            pltpu.VMEM((2, SIDE, 4, PER_OWNER, COLS), F32),
            pltpu.SemaphoreType.DMA((7,)),
            pltpu.SemaphoreType.DMA((2, SIDE)),
            pltpu.SemaphoreType.DMA((2, SIDE)),
            pltpu.SemaphoreType.DMA((2, 4)),
            pltpu.SemaphoreType.DMA((SIDE,)),
            pltpu.SemaphoreType.DMA((SIDE,)),
            pltpu.SemaphoreType.DMA((2, 4)),
            pltpu.SemaphoreType.DMA((2, 2, 4, 2)),
            pltpu.SemaphoreType.DMA((2, 2, 4, 2)),
        ],
        compiler_params=pltpu.CompilerParams(
            collective_id=0, has_side_effects=True, vmem_limit_bytes=62 << 20
        ),
    )(inputs, grad_out, momentum, listed, table)
    return (update, new_momentum[None])


def solution(mesh):
    return jax.shard_map(
        per_device,
        mesh=mesh,
        in_specs=(
            P("dp", None, None, None),
            P("dp", None, None, "mp"),
            P("dp", None, "mp"),
            P(None, None, None, "mp"),
        ),
        out_specs=(P(None, "mp"), P("dp", None, "mp")),
        check_vma=False,
    )
```

time: 195 us -> 58.3 us (0.30)
  waiting for transfers between devices: 163 us -> 0 us
  Pallas kernels: 0 us -> 53.1 us
  matrix products: 15.8 us -> 0 us
  between operations: 14.2 us -> 0.64 us
  local copies, waits for them, and re-layouts: 2.1 us -> 4.13 us
    psum x1 -> x0, waiting for transfers between devices: 163 us -> none  [per_device(): summed = lax.psum(sent_total, 'dp')]
    pallas_call x0 -> x1, Pallas kernels: none -> 53.1 us  [per_device(): pl.pallas_call(kernel, out_shape=(jax.ShapeDtypeStruct((ROWS, COLS), BF16...]
    dot_general x10 -> x0, matrix products: 15.8 us -> none  [the longest x2 4.33 us: inverse_blocks(): jnp.einsum('ui,auc->aic', dct_table, shaped, precision=lax.Precision.HIGH...]
    unnamed x5 -> x2, local copies, waits for them, and re-layouts: 0.54 us -> 4.13 us
  transfers between devices with their start and end apart: 1 -> 0, of which waited for: 1 -> 0; matrix products, arithmetic and copies ran while one was open for 2% -> 0% of each run, Pallas kernels for 0% -> 0%
where the time goes in v2:
time: 58.3 us; the launch traced here: 57.9 us
  Pallas kernels  53.1 us (91%)
  local copies, waits for them, and re-layouts  4.13 us (7%)
  between operations  0.64 us (1%)
    pallas_call x1, Pallas kernels, per_device(): pl.pallas_call(kernel, out_shape=(jax.ShapeDtypeStruct((ROWS, COLS), BF16...  53.1 us
    unnamed x2, local copies, waits for them, and re-layouts  4.13 us

profile of v2, /device:TPU:6, one launch (start us, length us, event | category | flops | bytes accessed | tf_op | source)
XLA Modules:
  0.0 57.9 jit_solution(1859952752932892973)
XLA Ops:
  0.6 53.1 %shard_map.68 = (bf16[2048,128]{1,0:T(8,128)(2,1)}, f32[2048,128]{1,0:T(8,128)}) custom-call(bf16[1,2,256,2048]{3,2,1,0:T(8,128)(2,1)} %x_hbm.1, bf16[1,2,256,128]{3,2,1,0:T(8,128)(2,1)} %g_hbm.1, f32[1,2048,128]{2,1,0:T(8,128)} %m_hbm.1, s32[64,2,8,64]{3,2,1,0:T(8,128)} %bitcast.3, bf16[1536,256]{1,0:T(8,128)(2,1)} %constant.2.clone.tab_hbm), custom_call_target="tpu_custom_call" | custom-call | tf_op jit(solution)/shard_map/pallas_call | solution.py:365
  53.8 1.9 %copy.9 = bf16[2048,128]{1,0:T(8,128)(2,1)} copy(bf16[2048,128]{1,0:T(8,128)(2,1)} %get-tuple-element.8) | data formatting | bytes 1048576
  55.6 2.3 %copy.10 = f32[1,2048,128]{2,1,0:T(8,128)} copy(f32[1,2048,128]{2,1,0:T(8,128)} %bitcast.2) | data formatting | bytes 2097152

commit v3 on v2

v3 whole, which is shorter than its diff:
```python
import jax
import jax.numpy as jnp
import numpy as np
from jax import lax
from jax.experimental import pallas as pl
from jax.experimental.pallas import tpu as pltpu
from jax.sharding import PartitionSpec as P

GROUP = 64
DECAY = 0.999
SIDE = 8
PER_OWNER = 32
CAP = 8
STEPS = 2
ROWS = 2048
COLS = 128
TOK = 256
SPAN = 256
BF16 = jnp.bfloat16
F32 = jnp.float32
MESH = pl.DeviceIdType.MESH
FAR_FIRST = (4, 3, 5, 2, 6, 1, 7)
NEAR_EVEN = (0, 2, -2, 4)
NEAR_ODD = (1, -1, 3, -3)


def transform_tables():
    u = np.arange(GROUP)[:, None].astype(np.float64)
    i = np.arange(GROUP)[None, :].astype(np.float64)
    scale = np.where(u == 0, np.sqrt(1.0 / GROUP), np.sqrt(2.0 / GROUP))
    dct = (scale * np.cos(np.pi * (2 * i + 1) * u / (2 * GROUP))).astype(np.float32)
    rows = np.kron(np.eye(SPAN // GROUP, dtype=np.float32), dct)

    def by_row(table):
        high = table.astype(BF16)
        low = (table - high.astype(np.float32)).astype(BF16)
        return np.concatenate([high, low], 0)

    return np.concatenate([by_row(rows), by_row(rows.T)], 0)


TABLE_ROWS = 1024


def split(x):
    high = x.astype(BF16)
    low = (x - high.astype(F32)).astype(BF16)
    return jnp.concatenate([high, low], axis=1)


def dot(a, b, dims=(((1,), (0,)), ((), ()))):
    return lax.dot_general(a, b, dims, preferred_element_type=F32)


def folded(x):
    return x[:, :COLS] + x[:, COLS:]


def row_apply(table, x):
    r = dot(table, split(x))
    return r[:SPAN, :COLS] + (r[:SPAN, COLS:] + r[SPAN:, :COLS])


def kernel(
    x_hbm, g_hbm, m_hbm, sel_hbm, tab_hbm,
    upd_ref, mom_ref,
    x_v, g_v, m_v, sel_v, tab_v, f_v, kept_v,
    zsend, ysend, zin, yin, pz, py, p2in, tout, u_v,
    load_sem, r1s, r1r, p2s, p2r, a1s, a1r, a2s, a2r,
):
    me = lax.axis_index("dp")
    mp = lax.axis_index("mp")
    y = me // SIDE
    z = me % SIDE
    par = (y + z) % 2

    def at(yy, zz):
        return (yy * SIDE + zz, mp)

    loads = []

    def load(src, dst):
        copy = pltpu.make_async_copy(src, dst, load_sem.at[len(loads)])
        copy.start()
        loads.append(copy)
        return copy

    load_g = load(g_hbm.at[0], g_v)
    load_tab = load(tab_hbm.at[pl.ds(0, 512)], tab_v.at[pl.ds(0, 512)])
    load_x0 = load(x_hbm.at[0, 0], x_v.at[0])
    load_m = load(m_hbm.at[0], m_v)
    load_sel = load(sel_hbm, sel_v)
    load_x1 = load(x_hbm.at[0, 1], x_v.at[1])
    load_tab2 = load(tab_hbm.at[pl.ds(512, 512)], tab_v.at[pl.ds(512, 512)])

    barrier = pltpu.get_barrier_semaphore()
    for d in range(1, SIDE):
        pl.semaphore_signal(barrier, inc=1, device_id=at((y + d) % SIDE, z), device_id_type=MESH)
        pl.semaphore_signal(barrier, inc=1, device_id=at(y, (z + d) % SIDE), device_id_type=MESH)

    tn = (((0,), (0,)), ((), ()))
    load_g.wait()
    load_x0.wait()
    load_m.wait()
    for g in range(SIDE):
        rows = pl.ds(g * SPAN, SPAN)
        f_v[0, g] = DECAY * m_v[rows, :] + dot(x_v[0, :, rows], g_v[0], tn)
    load_x1.wait()
    for g in range(SIDE):
        rows = pl.ds(g * SPAN, SPAN)
        f_v[1, g] = dot(x_v[1, :, rows], g_v[1], tn)

    load_tab.wait()
    load_sel.wait()
    lane = lax.broadcasted_iota(jnp.int32, (CAP, SPAN), 1)
    ones = jnp.ones((SIDE * CAP, COLS), BF16)
    owner_lane = lax.broadcasted_iota(jnp.int32, (CAP, SIDE * SIDE), 1)
    forward = tab_v[0:512, :]
    for s in range(STEPS):
        own = sel_v[me, s]
        own = jnp.where(own >= 0, own + (owner_lane % SIDE) * PER_OWNER, -1)
        for g in range(SIDE):
            c = row_apply(forward, f_v[s, g])
            if s:
                c = c + DECAY * kept_v[g]
            picks = [
                (own[:, g * SIDE + q : g * SIDE + q + 1] == lane).astype(F32)
                for q in range(SIDE)
            ]
            onehot = jnp.concatenate(picks, axis=0).astype(BF16)
            mask = dot(onehot, ones, tn)
            packed = folded(dot(onehot, split(c)))
            kept_v[g] = jnp.where(mask > 0.5, 0.0, c)
            for q in range(SIDE):
                tile = packed[q * CAP : (q + 1) * CAP]
                if (g + q) % 2 == 0:
                    zsend[q, g // 2, s * CAP : (s + 1) * CAP, :] = tile
                else:
                    ysend[g, q // 2, s * CAP : (s + 1) * CAP, :] = tile

    pl.semaphore_wait(barrier, 2 * (SIDE - 1))
    def first(axis, d):
        if axis == 0:
            to = (z + d) % SIDE
            return pltpu.make_async_remote_copy(
                src_ref=zsend.at[to], dst_ref=zin.at[z],
                send_sem=r1s.at[0, d], recv_sem=r1r.at[0, d],
                device_id=at(y, to), device_id_type=MESH,
            )
        to = (y + d) % SIDE
        return pltpu.make_async_remote_copy(
            src_ref=ysend.at[to], dst_ref=yin.at[y],
            send_sem=r1s.at[1, d], recv_sem=r1r.at[1, d],
            device_id=at(to, z), device_id_type=MESH,
        )

    for d in FAR_FIRST:
        for axis in range(2):
            first(axis, d).start()
    zin[z] = zsend[z]
    yin[y] = ysend[y]

    load_tab2.wait()
    pick_row = lax.broadcasted_iota(jnp.int32, (COLS, SIDE * SIDE), 0)
    pick_lane = lax.broadcasted_iota(jnp.int32, (COLS, SIDE * SIDE), 1)
    place = (lax.broadcasted_iota(jnp.int32, (COLS, COLS), 0) % PER_OWNER).astype(F32)
    nt = (((1,), (1,)), ((), ()))

    def scatter_table(listed, owner):
        chooser = (pick_lane == owner).astype(F32).astype(BF16)
        wanted = dot(chooser, listed.astype(F32).astype(BF16), nt)
        return (wanted == place).astype(F32).astype(BF16)

    along_z = sel_v[pl.ds(y * SIDE, SIDE)].reshape(COLS, SIDE * SIDE)
    along_y = jnp.concatenate(
        [sel_v[q * SIDE + z].reshape(STEPS * CAP, SIDE * SIDE) for q in range(SIDE)], axis=0
    )
    index = pick_row // PER_OWNER
    table_z = scatter_table(along_z, (2 * index + z % 2) * SIDE + z)
    table_y = scatter_table(along_y, y * SIDE + 2 * index + (y + 1) % 2)

    backward = tab_v[512:1024, :]
    for g in range(SIDE):
        mom_ref[g * SPAN : (g + 1) * SPAN, :] = row_apply(backward, kept_v[g])

    for d in FAR_FIRST:
        for axis in range(2):
            first(axis, d).wait_recv()
    for i in range(4):
        block = slice(i * PER_OWNER, (i + 1) * PER_OWNER)
        pz[i] = folded(dot(table_z[block], split(zin[:, i].reshape(COLS, COLS))))
        py[i] = folded(dot(table_y[block], split(yin[:, i].reshape(COLS, COLS))))

    def done1():
        for d in FAR_FIRST:
            for axis in range(2):
                first(axis, d).wait_send()
    def peer(axis, k):
        far = par if axis == 0 else 1 - par
        offset = NEAR_EVEN[k] + far * (NEAR_ODD[k] - NEAR_EVEN[k])
        return far, ((y if axis == 0 else z) + offset + SIDE) % SIDE

    def second(axis, k):
        _, to = peer(axis, k)
        return pltpu.make_async_remote_copy(
            src_ref=(pz if axis == 0 else py).at[to // 2],
            dst_ref=p2in.at[y if axis == 0 else z],
            send_sem=p2s.at[axis, k], recv_sem=p2r.at[y if axis == 0 else z],
            device_id=at(to, z) if axis == 0 else at(y, to), device_id_type=MESH,
        )

    for k in (3, 2, 1):
        for axis in range(2):
            second(axis, k).start()
    along = y + par * (z - y)
    line = z + par * (y - z)
    mine = along // 2
    for axis in range(2):
        far, _ = peer(axis, 0)

        @pl.when(far == 1)
        def _():
            second(axis, 0).start()

        @pl.when(far == 0)
        def _():
            p2in[along] = (pz if axis == 0 else py)[mine]

    total = p2in[along]
    for d in (1, 7, 2, 6, 3, 5, 4):
        source = (along + d) % SIDE
        pltpu.make_async_remote_copy(
            src_ref=pz.at[0], dst_ref=p2in.at[source],
            send_sem=p2s.at[0, 0], recv_sem=p2r.at[source],
            device_id=at((y + 1) % SIDE, z), device_id_type=MESH,
        ).wait_recv()
        total = total + p2in[source]
    tout[...] = total
    u_v[par, line, mine] = total

    def done2():
        done1()
        for axis in range(2):
            for k in (3, 2, 1):
                second(axis, k).wait_send()
            far, _ = peer(axis, 0)

            @pl.when(far == 1)
            def _():
                second(axis, 0).wait_send()

    def third(d):
        to_y = (y + (1 - par) * d) % SIDE
        to_z = (z + par * d) % SIDE
        return pltpu.make_async_remote_copy(
            src_ref=tout, dst_ref=u_v.at[par, line, mine],
            send_sem=a1s.at[d], recv_sem=a1r.at[par, mine],
            device_id=at(to_y, to_z), device_id_type=MESH,
        )

    for d in FAR_FIRST:
        third(d).start()

    def third_arrived(axis, k):
        far, source = peer(axis, k)
        where = z if axis == 0 else y

        def wait():
            pltpu.make_async_remote_copy(
                src_ref=tout, dst_ref=u_v.at[axis, where, source // 2],
                send_sem=a1s.at[1], recv_sem=a1r.at[axis, source // 2],
                device_id=at((y + 1) % SIDE, z), device_id_type=MESH,
            ).wait_recv()

        if k:
            wait()
        else:
            pl.when(far == 1)(wait)
        return source // 2

    def spread(axis, way, hop, behind, i):
        pos = z if axis == 0 else y
        step = 1 if way == 0 else SIDE - 1
        source = (pos + behind * (SIDE - step)) % SIDE
        to = (pos + hop * step) % SIDE
        block = u_v.at[axis, source, i]
        slot = 2 * (behind + hop - 1) + way
        return pltpu.make_async_remote_copy(
            src_ref=block, dst_ref=block,
            send_sem=a2s.at[axis, slot, i], recv_sem=a2r.at[axis, slot, i],
            device_id=at(y, to) if axis == 0 else at(to, z), device_id_type=MESH,
        )

    def spread_arrived(axis, way, distance, i):
        pos = z if axis == 0 else y
        step = 1 if way == 0 else SIDE - 1
        source = (pos + distance * (SIDE - step)) % SIDE
        block = u_v.at[axis, source, i]
        slot = 2 * (distance - 1) + way
        pltpu.make_async_remote_copy(
            src_ref=block, dst_ref=block,
            send_sem=a2s.at[axis, slot, i], recv_sem=a2r.at[axis, slot, i],
            device_id=at((y + 1) % SIDE, z), device_id_type=MESH,
        ).wait_recv()

    order = {}
    for k in range(4):
        for axis in range(2):
            i = third_arrived(axis, k)
            order[axis, k] = i
            for way in range(2):
                spread(axis, way, 2, 0, i).start()
    for k in range(4):
        for axis in range(2):
            for way in range(2):
                spread(axis, way, 1, 0, order[axis, k]).start()
    for k in range(4):
        for axis in range(2):
            i = order[axis, k]
            for way in range(2):
                spread_arrived(axis, way, 2, i)

                @pl.when(i // 2 == way)
                def _():
                    spread(axis, way, 2, 2, i).start()

                spread(axis, way, 1, 2, i).start()
    for axis in range(2):
        for way in range(2):
            for i in range(4):
                spread_arrived(axis, way, 1, i)
    for axis in range(2):
        for way in range(2):
            for i in range(4):
                spread_arrived(axis, way, 3, i)
                if i // 2 == way:
                    spread_arrived(axis, way, 4, i)

    for g in range(SIDE):
        parts = [
            u_v[0, q, g // 2] if (g + q) % 2 == 0 else u_v[1, g, q // 2] for q in range(SIDE)
        ]
        block = row_apply(backward, jnp.concatenate(parts, axis=0))
        upd_ref[g * SPAN : (g + 1) * SPAN, :] = block.astype(BF16)

    done2()
    for d in FAR_FIRST:
        third(d).wait_send()
    for axis in range(2):
        for way in range(2):
            for i in range(4):
                spread(axis, way, 2, 0, i).wait_send()
                spread(axis, way, 1, 0, i).wait_send()
                spread(axis, way, 1, 2, i).wait_send()
                if i // 2 == way:
                    spread(axis, way, 2, 2, i).wait_send()


def deliver(upd_ref, mom_ref, upd_out, mom_out, sem):
    first = pltpu.make_async_copy(mom_ref, mom_out, sem.at[0])
    second = pltpu.make_async_copy(upd_ref, upd_out, sem.at[1])
    first.start()
    second.start()
    first.wait()
    second.wait()


def per_device(inputs, grad_out, momentum, select):
    table = jnp.asarray(transform_tables())
    listed = jnp.transpose(select, (0, 1, 3, 2))
    hbm = pl.BlockSpec(memory_space=pl.ANY)
    vmem = pl.BlockSpec(memory_space=pltpu.VMEM)
    operands = [
        pltpu.with_memory_space_constraint(v, pltpu.HBM)
        for v in (inputs, grad_out, momentum, listed, table)
    ]
    outs = (
        jax.ShapeDtypeStruct((ROWS, COLS), BF16),
        jax.ShapeDtypeStruct((ROWS, COLS), F32),
    )
    update, new_momentum = pl.pallas_call(
        kernel,
        out_shape=outs,
        in_specs=[hbm] * 5,
        out_specs=(vmem, vmem),
        scratch_shapes=[
            pltpu.VMEM((STEPS, TOK, ROWS), BF16),
            pltpu.VMEM((STEPS, TOK, COLS), BF16),
            pltpu.VMEM((ROWS, COLS), F32),
            pltpu.VMEM((SIDE * SIDE, STEPS, CAP, SIDE * SIDE), jnp.int32),
            pltpu.VMEM((TABLE_ROWS, SPAN), BF16),
            pltpu.VMEM((STEPS, SIDE, SPAN, COLS), F32),
            pltpu.VMEM((SIDE, SPAN, COLS), F32),
            pltpu.VMEM((SIDE, 4, STEPS * CAP, COLS), F32),
            pltpu.VMEM((SIDE, 4, STEPS * CAP, COLS), F32),
            pltpu.VMEM((SIDE, 4, STEPS * CAP, COLS), F32),
            pltpu.VMEM((SIDE, 4, STEPS * CAP, COLS), F32),
            pltpu.VMEM((4, PER_OWNER, COLS), F32),
            pltpu.VMEM((4, PER_OWNER, COLS), F32),
            pltpu.VMEM((SIDE, PER_OWNER, COLS), F32),
            pltpu.VMEM((PER_OWNER, COLS), F32),
            pltpu.VMEM((2, SIDE, 4, PER_OWNER, COLS), F32),
            pltpu.SemaphoreType.DMA((7,)),
            pltpu.SemaphoreType.DMA((2, SIDE)),
            pltpu.SemaphoreType.DMA((2, SIDE)),
            pltpu.SemaphoreType.DMA((2, 4)),
            pltpu.SemaphoreType.DMA((SIDE,)),
            pltpu.SemaphoreType.DMA((SIDE,)),
            pltpu.SemaphoreType.DMA((2, 4)),
            pltpu.SemaphoreType.DMA((2, 8, 4)),
            pltpu.SemaphoreType.DMA((2, 8, 4)),
        ],
        compiler_params=pltpu.CompilerParams(
            collective_id=0, has_side_effects=True, vmem_limit_bytes=40 << 20
        ),
    )(*operands)
    update, new_momentum = pl.pallas_call(
        deliver,
        out_shape=outs,
        in_specs=[hbm] * 2,
        out_specs=(hbm, hbm),
        scratch_shapes=[pltpu.SemaphoreType.DMA((2,))],
        compiler_params=pltpu.CompilerParams(vmem_limit_bytes=8 << 20),
    )(update, new_momentum)
    return (update, new_momentum[None])


def solution(mesh):
    return jax.shard_map(
        per_device,
        mesh=mesh,
        in_specs=(
            P("dp", None, None, None),
            P("dp", None, None, "mp"),
            P("dp", None, "mp"),
            P(None, None, None, "mp"),
        ),
        out_specs=(P(None, "mp"), P("dp", None, "mp")),
        check_vma=False,
    )
```

time: 58.3 us -> 49.3 us (0.85)
  Pallas kernels: 53.1 us -> 48.5 us
  local copies, waits for them, and re-layouts: 4.13 us -> 0 us
    pallas_call x1 -> x2, Pallas kernels: 53.1 us -> 48.5 us  [the longest x1 47.4 us: per_device(): pl.pallas_call(kernel, out_shape=outs, in_specs=[hbm] * 5, out_specs=(vme...]
    unnamed x2 -> x0, local copies, waits for them, and re-layouts: 4.13 us -> none
where the time goes in v3:
time: 49.3 us; the launch traced here: 49.2 us
  Pallas kernels  48.5 us (98%)
  between operations  0.64 us (1%)
    pallas_call x1, Pallas kernels, per_device(): pl.pallas_call(kernel, out_shape=outs, in_specs=[hbm] * 5, out_specs=(vme...  47.4 us
    pallas_call x1, Pallas kernels, per_device(): pl.pallas_call(deliver, out_shape=outs, in_specs=[hbm] * 2, out_specs=(hb...  1.16 us

profile of v3, /device:TPU:6, one launch (start us, length us, event | category | flops | bytes accessed | tf_op | source)
XLA Modules:
  0.0 49.2 jit_solution(13333390638443636840)
XLA Ops:
  0.6 47.4 %shard_map.68 = (bf16[2048,128]{1,0:T(8,128)(2,1)S(1)}, f32[2048,128]{1,0:T(8,128)S(1)}) custom-call(bf16[1,2,256,2048]{3,2,1,0:T(8,128)(2,1)} %x_hbm.1, bf16[1,2,256,128]{3,2,1,0:T(8,128)(2,1)} %g_hbm.1, f32[1,2048,128]{2,1,0:T(8,128)} %m_hbm.1, s32[64,2,8,64]{3,2,1,0:T(8,128)} %bitcast.2, bf16[1024,256]{1,0:T(8,128)(2,1)} %constant.2.clone.tab_hbm), custom_call_target="tpu_custom_call" | custom-call | tf_op jit(solution)/shard_map/pallas_call | solution.py:381
  48.0 1.2 %shard_map.69 = (bf16[2048,128]{1,0:T(8,128)(2,1)}, f32[2048,128]{1,0:T(8,128)}) custom-call(bf16[2048,128]{1,0:T(8,128)(2,1)S(1)} %get-tuple-element.6.upd_ref, f32[2048,128]{1,0:T(8,128)S(1)} %get-tuple-element.7.mom_ref), custom_call_target="tpu_custom_call" | custom-call | tf_op jit(solution)/shard_map/pallas_call | solution.py:417

commit v4 on v3

v4 whole, which is shorter than its diff:
```python
import jax
import jax.numpy as jnp
import numpy as np
from jax import lax
from jax.experimental import pallas as pl
from jax.experimental.pallas import tpu as pltpu
from jax.sharding import PartitionSpec as P

GROUP = 64
DECAY = 0.999
SIDE = 8
PER_OWNER = 32
CAP = 8
STEPS = 2
ROWS = 2048
COLS = 128
TOK = 256
SPAN = 256
BF16 = jnp.bfloat16
F32 = jnp.float32
MESH = pl.DeviceIdType.MESH
FAR_FIRST = (4, 3, 5, 2, 6, 1, 7)
NEAR_EVEN = (0, 2, -2, 4)
NEAR_ODD = (1, -1, 3, -3)


def transform_tables():
    u = np.arange(GROUP)[:, None].astype(np.float64)
    i = np.arange(GROUP)[None, :].astype(np.float64)
    scale = np.where(u == 0, np.sqrt(1.0 / GROUP), np.sqrt(2.0 / GROUP))
    dct = (scale * np.cos(np.pi * (2 * i + 1) * u / (2 * GROUP))).astype(np.float32)

    def parts(table):
        high = table.astype(BF16)
        low = (table - high.astype(np.float32)).astype(BF16)
        return np.concatenate([high, high, low, low], 1)

    return np.concatenate([parts(dct), parts(dct.T)], 0)


def split(x):
    high = x.astype(BF16)
    low = (x - high.astype(F32)).astype(BF16)
    return jnp.concatenate([high, low], axis=1)


def dot(a, b, dims=(((1,), (0,)), ((), ()))):
    return lax.dot_general(a, b, dims, preferred_element_type=F32)


def folded(x):
    return x[:, :COLS] + x[:, COLS:]


def blocks_apply(table, x):
    high = x.astype(BF16)
    low = (x - high.astype(F32)).astype(BF16)

    def stacked(b):
        rows = slice(b * GROUP, (b + 1) * GROUP)
        return jnp.concatenate([high[rows], low[rows]], axis=0)

    out = []
    for b in range(0, SPAN // GROUP, 2):
        pair = jnp.concatenate([stacked(b), stacked(b + 1)], axis=1)
        r = dot(table, jnp.concatenate([pair, pair], axis=0))
        out += [r[:, :COLS], r[:, COLS:]]
    return jnp.concatenate(out, axis=0)


CHUNKS = 2
HALVES = 2
PER_CHUNK = 4 // CHUNKS


def kernel(
    x_hbm, g_hbm, m_hbm, sel_hbm, tab_hbm,
    u_v, mom_ref, back_v,
    x_v, g_v, m_v, sel_v, own_v, tab_v, f_v, kept_v, pick_v, keep_v,
    zsend, ysend, zin, yin, pz, py, p2in, tout,
    load_sem, r1s, r1r, p2s, p2r, a1s, a1r, a2s, a2r,
):
    me = lax.axis_index("dp")
    mp = lax.axis_index("mp")
    y = me // SIDE
    z = me % SIDE
    par = (y + z) % 2

    def at(yy, zz):
        return (yy * SIDE + zz, mp)

    loads = []

    def load(src, dst):
        copy = pltpu.make_async_copy(src, dst, load_sem.at[len(loads)])
        copy.start()
        loads.append(copy)
        return copy

    half_rows = ROWS // HALVES
    load_own = load(sel_hbm.at[me], own_v)
    load_g = load(g_hbm.at[0], g_v)
    load_tab = load(tab_hbm.at[pl.ds(0, GROUP)], tab_v)
    load_half = []
    for half in range(HALVES):
        rows = pl.ds(half * half_rows, half_rows)
        load_half.append(
            [
                load(x_hbm.at[0, 0, :, rows], x_v.at[0, :, rows]),
                load(m_hbm.at[0, rows], m_v.at[rows]),
                load(x_hbm.at[0, 1, :, rows], x_v.at[1, :, rows]),
            ]
        )
    load_sel = load(sel_hbm, sel_v)
    load_back = load(tab_hbm.at[pl.ds(GROUP, GROUP)], back_v)

    barrier = pltpu.get_barrier_semaphore()
    for d in range(1, SIDE):
        pl.semaphore_signal(barrier, inc=1, device_id=at((y + d) % SIDE, z), device_id_type=MESH)
        pl.semaphore_signal(barrier, inc=1, device_id=at(y, (z + d) % SIDE), device_id_type=MESH)

    def first(axis, d, c):
        part = pl.ds(c * PER_CHUNK, PER_CHUNK)
        to = ((z if axis == 0 else y) + d) % SIDE
        return pltpu.make_async_remote_copy(
            src_ref=(zsend if axis == 0 else ysend).at[to, part],
            dst_ref=(zin if axis == 0 else yin).at[z if axis == 0 else y, part],
            send_sem=r1s.at[axis], recv_sem=r1r.at[axis, c],
            device_id=at(y, to) if axis == 0 else at(to, z), device_id_type=MESH,
        )

    tn = (((0,), (0,)), ((), ()))
    lane = lax.broadcasted_iota(jnp.int32, (CAP, SPAN), 1)
    ones = jnp.ones((SIDE * CAP, COLS), BF16)
    owner_lane = lax.broadcasted_iota(jnp.int32, (CAP, SIDE * SIDE), 1)
    load_own.wait()
    for s in range(STEPS):
        own = own_v[s]
        own = jnp.where(own >= 0, own + (owner_lane % SIDE) * PER_OWNER, -1)
        for g in range(SIDE):
            picks = [
                (own[:, g * SIDE + q : g * SIDE + q + 1] == lane).astype(F32)
                for q in range(SIDE)
            ]
            onehot = jnp.concatenate(picks, axis=0).astype(BF16)
            pick_v[s, g] = onehot
            keep_v[s, g] = 1.0 - dot(onehot, ones, tn)
    load_g.wait()
    load_tab.wait()
    for half in range(HALVES):
        groups = range(half * SIDE // HALVES, (half + 1) * SIDE // HALVES)
        load_half[half][0].wait()
        load_half[half][1].wait()
        for g in groups:
            rows = pl.ds(g * SPAN, SPAN)
            f_v[0, g] = DECAY * m_v[rows, :] + dot(x_v[0, :, rows], g_v[0], tn)
        load_half[half][2].wait()
        for g in groups:
            rows = pl.ds(g * SPAN, SPAN)
            f_v[1, g] = dot(x_v[1, :, rows], g_v[1], tn)
        for s in range(STEPS):
            for g in groups:
                c = blocks_apply(tab_v[...], f_v[s, g])
                if s:
                    c = c + DECAY * kept_v[g]
                packed = folded(dot(pick_v[s, g], split(c)))
                kept_v[g] = keep_v[s, g] * c
                for q in range(SIDE):
                    tile = packed[q * CAP : (q + 1) * CAP]
                    if (g + q) % 2 == 0:
                        zsend[q, g // 2, s * CAP : (s + 1) * CAP, :] = tile
                    else:
                        ysend[g, q // 2, s * CAP : (s + 1) * CAP, :] = tile
        if half == 0:
            pl.semaphore_wait(barrier, 2 * (SIDE - 1))
        for c in range(CHUNKS):
            if c * HALVES // CHUNKS == half:
                for d in FAR_FIRST:
                    first(0, d, c).start()
        if HALVES == 1:
            for c in range(CHUNKS):
                for d in FAR_FIRST:
                    first(1, d, c).start()
        else:
            for c in range(CHUNKS):
                for g in groups:

                    @pl.when(y != g)
                    def _():
                        first(1, (g - y + SIDE) % SIDE, c).start()

    zin[z] = zsend[z]
    yin[y] = ysend[y]

    load_sel.wait()
    load_back.wait()
    pick_row = lax.broadcasted_iota(jnp.int32, (COLS, SIDE * SIDE), 0)
    pick_lane = lax.broadcasted_iota(jnp.int32, (COLS, SIDE * SIDE), 1)
    place = (lax.broadcasted_iota(jnp.int32, (COLS, COLS), 0) % PER_OWNER).astype(F32)
    nt = (((1,), (1,)), ((), ()))

    def scatter_table(listed, owner):
        chooser = (pick_lane == owner).astype(F32).astype(BF16)
        wanted = dot(chooser, listed.astype(F32).astype(BF16), nt)
        return (wanted == place).astype(F32).astype(BF16)

    along_z = sel_v[pl.ds(y * SIDE, SIDE)].reshape(COLS, SIDE * SIDE)
    along_y = jnp.concatenate(
        [sel_v[q * SIDE + z].reshape(STEPS * CAP, SIDE * SIDE) for q in range(SIDE)], axis=0
    )
    index = pick_row // PER_OWNER
    table_z = scatter_table(along_z, (2 * index + z % 2) * SIDE + z)
    table_y = scatter_table(along_y, y * SIDE + 2 * index + (y + 1) % 2)

    backward = back_v[...]
    for g in range(SIDE):
        mom_ref[g * SPAN : (g + 1) * SPAN, :] = blocks_apply(backward, kept_v[g])

    def second(axis, i):
        to = 2 * i + (z % 2 if axis == 0 else (y + 1) % 2)
        return to, pltpu.make_async_remote_copy(
            src_ref=(pz if axis == 0 else py).at[i],
            dst_ref=p2in.at[y if axis == 0 else z],
            send_sem=p2s, recv_sem=p2r,
            device_id=at(to, z) if axis == 0 else at(y, to), device_id_type=MESH,
        )

    def others(ref, send_sem, recv_sem):
        return pltpu.make_async_remote_copy(
            src_ref=ref, dst_ref=ref, send_sem=send_sem, recv_sem=recv_sem,
            device_id=at((y + 1) % SIDE, z), device_id_type=MESH,
        )

    def await_recv(ref, sem):
        others(ref, p2s, sem).wait_recv()

    def await_send(ref, sem):
        others(ref, sem, p2r).wait_send()

    for c in range(CHUNKS):
        part = pl.ds(c * PER_CHUNK, PER_CHUNK)
        for axis in range(2):
            await_recv((zin if axis == 0 else yin).at[pl.ds(0, SIDE - 1), part], r1r.at[axis, c])
        for i in range(c * PER_CHUNK, (c + 1) * PER_CHUNK):
            block = slice(i * PER_OWNER, (i + 1) * PER_OWNER)
            for axis in range(2):
                arrived = (zin if axis == 0 else yin)[:, i].reshape(COLS, COLS)
                table = table_z if axis == 0 else table_y
                (pz if axis == 0 else py)[i] = folded(dot(table[block], split(arrived)))
        for i in range(c * PER_CHUNK, (c + 1) * PER_CHUNK):
            for axis in range(2):
                to, copy = second(axis, i)
                here = y if axis == 0 else z

                @pl.when(to != here)
                def _():
                    copy.start()

                @pl.when(to == here)
                def _():
                    p2in[here] = (pz if axis == 0 else py)[i]

    def done1():
        await_send(zsend.at[pl.ds(0, SIDE - 1)], r1s.at[0])
        await_send(ysend.at[pl.ds(0, SIDE - 1)], r1s.at[1])

    along = y + par * (z - y)
    line = z + par * (y - z)
    mine = along // 2
    await_recv(p2in.at[pl.ds(0, SIDE - 1)], p2r)
    total = p2in[0]
    for k in range(1, SIDE):
        total = total + p2in[k]
    tout[...] = total
    u_v[par, line, mine] = total

    def done2():
        done1()
        await_send(p2in.at[pl.ds(0, SIDE - 1)], p2s)

    def third(d):
        to_y = (y + (1 - par) * d) % SIDE
        to_z = (z + par * d) % SIDE
        return pltpu.make_async_remote_copy(
            src_ref=tout, dst_ref=u_v.at[par, line, mine],
            send_sem=a1s, recv_sem=a1r.at[par, mine],
            device_id=at(to_y, to_z), device_id_type=MESH,
        )

    for d in FAR_FIRST:
        third(d).start()

    def third_arrived(axis, i):
        where = z if axis == 0 else y

        @pl.when(jnp.logical_or(par != axis, mine != i))
        def _():
            await_recv(u_v.at[axis, where, i], a1r.at[axis, i])

    def spread(axis, way, hop, behind, first_block, blocks):
        pos = z if axis == 0 else y
        step = 1 if way == 0 else SIDE - 1
        source = (pos + behind * (SIDE - step)) % SIDE
        to = (pos + hop * step) % SIDE
        block = u_v.at[axis, source, pl.ds(first_block, blocks)]
        slot = 2 * (behind + hop - 1) + way
        return pltpu.make_async_remote_copy(
            src_ref=block, dst_ref=block,
            send_sem=a2s.at[axis], recv_sem=a2r.at[axis, slot, first_block // 2],
            device_id=at(y, to) if axis == 0 else at(to, z), device_id_type=MESH,
        )

    def spread_arrived(axis, way, distance, first_block, blocks):
        pos = z if axis == 0 else y
        step = 1 if way == 0 else SIDE - 1
        source = (pos + distance * (SIDE - step)) % SIDE
        block = u_v.at[axis, source, pl.ds(first_block, blocks)]
        await_recv(block, a2r.at[axis, 2 * (distance - 1) + way, first_block // 2])

    for half in range(2):
        for axis in range(2):
            for i in (2 * half, 2 * half + 1):
                third_arrived(axis, i)
            for way in range(2):
                spread(axis, way, 2, 0, 2 * half, 2).start()
    for axis in range(2):
        for way in range(2):
            spread(axis, way, 1, 0, 0, 4).start()
    for half in range(2):
        for axis in range(2):
            for way in range(2):
                spread_arrived(axis, way, 2, 2 * half, 2)
                if half == way:
                    spread(axis, way, 2, 2, 2 * half, 2).start()
                spread(axis, way, 1, 2, 2 * half, 2).start()
    done2()
    await_send(p2in.at[pl.ds(0, SIDE - 1)], a1s)
    for axis in range(2):
        for way in range(2):
            spread_arrived(axis, way, 1, 0, 4)
    for half in range(2):
        for axis in range(2):
            for way in range(2):
                spread_arrived(axis, way, 3, 2 * half, 2)
                if half == way:
                    spread_arrived(axis, way, 4, 2 * half, 2)
    for axis in range(2):
        await_send(u_v.at[axis, pl.ds(0, SIDE - 1)], a2s.at[axis])


def deliver(u_ref, mom_ref, back_ref, upd_out, mom_out, upd_v, sem):
    momentum = pltpu.make_async_copy(mom_ref, mom_out, sem.at[SIDE])
    momentum.start()
    copies = []
    for g in range(SIDE):
        rows = pl.ds(g * SPAN, SPAN)
        parts = [
            u_ref[0, q, g // 2] if (g + q) % 2 == 0 else u_ref[1, g, q // 2]
            for q in range(SIDE)
        ]
        block = blocks_apply(back_ref[...], jnp.concatenate(parts, axis=0))
        upd_v[rows, :] = block.astype(BF16)
        copies.append(pltpu.make_async_copy(upd_v.at[rows], upd_out.at[rows], sem.at[g]))
        copies[-1].start()
    for copy in copies:
        copy.wait()
    momentum.wait()


def per_device(inputs, grad_out, momentum, select):
    table = jnp.asarray(transform_tables())
    listed = jnp.transpose(select, (0, 1, 3, 2))
    hbm = pl.BlockSpec(memory_space=pl.ANY)
    vmem = pl.BlockSpec(memory_space=pltpu.VMEM)
    operands = [
        pltpu.with_memory_space_constraint(v, pltpu.HBM)
        for v in (inputs, grad_out, momentum, listed, table)
    ]
    outs = (
        jax.ShapeDtypeStruct((ROWS, COLS), BF16),
        jax.ShapeDtypeStruct((ROWS, COLS), F32),
    )
    gathered, new_momentum, back = pl.pallas_call(
        kernel,
        out_shape=(
            jax.ShapeDtypeStruct((2, SIDE, 4, PER_OWNER, COLS), F32),
            outs[1],
            jax.ShapeDtypeStruct((GROUP, SPAN), BF16),
        ),
        in_specs=[hbm] * 5,
        out_specs=(vmem, vmem, vmem),
        scratch_shapes=[
            pltpu.VMEM((STEPS, TOK, ROWS), BF16),
            pltpu.VMEM((STEPS, TOK, COLS), BF16),
            pltpu.VMEM((ROWS, COLS), F32),
            pltpu.VMEM((SIDE * SIDE, STEPS, CAP, SIDE * SIDE), jnp.int32),
            pltpu.VMEM((STEPS, CAP, SIDE * SIDE), jnp.int32),
            pltpu.VMEM((GROUP, SPAN), BF16),
            pltpu.VMEM((STEPS, SIDE, SPAN, COLS), F32),
            pltpu.VMEM((SIDE, SPAN, COLS), F32),
            pltpu.VMEM((STEPS, SIDE, SIDE * CAP, SPAN), BF16),
            pltpu.VMEM((STEPS, SIDE, SPAN, COLS), F32),
            pltpu.VMEM((SIDE, 4, STEPS * CAP, COLS), F32),
            pltpu.VMEM((SIDE, 4, STEPS * CAP, COLS), F32),
            pltpu.VMEM((SIDE, 4, STEPS * CAP, COLS), F32),
            pltpu.VMEM((SIDE, 4, STEPS * CAP, COLS), F32),
            pltpu.VMEM((4, PER_OWNER, COLS), F32),
            pltpu.VMEM((4, PER_OWNER, COLS), F32),
            pltpu.VMEM((SIDE, PER_OWNER, COLS), F32),
            pltpu.VMEM((PER_OWNER, COLS), F32),
            pltpu.SemaphoreType.DMA((5 + 3 * HALVES,)),
            pltpu.SemaphoreType.DMA((2,)),
            pltpu.SemaphoreType.DMA((2, CHUNKS)),
            pltpu.SemaphoreType.DMA,
            pltpu.SemaphoreType.DMA,
            pltpu.SemaphoreType.DMA,
            pltpu.SemaphoreType.DMA((2, 4)),
            pltpu.SemaphoreType.DMA((2,)),
            pltpu.SemaphoreType.DMA((2, 8, 2)),
        ],
        compiler_params=pltpu.CompilerParams(
            collective_id=0, has_side_effects=True, vmem_limit_bytes=40 << 20
        ),
    )(*operands)
    update, new_momentum = pl.pallas_call(
        deliver,
        out_shape=outs,
        in_specs=[vmem] * 3,
        out_specs=(hbm, hbm),
        scratch_shapes=[
            pltpu.VMEM((ROWS, COLS), BF16),
            pltpu.SemaphoreType.DMA((SIDE + 1,)),
        ],
        compiler_params=pltpu.CompilerParams(vmem_limit_bytes=16 << 20),
    )(gathered, new_momentum, back)
    return (update, new_momentum[None])


def solution(mesh):
    return jax.shard_map(
        per_device,
        mesh=mesh,
        in_specs=(
            P("dp", None, None, None),
            P("dp", None, None, "mp"),
            P("dp", None, "mp"),
            P(None, None, None, "mp"),
        ),
        out_specs=(P(None, "mp"), P("dp", None, "mp")),
        check_vma=False,
    )
```

time: 49.3 us -> 45 us (0.913)
  Pallas kernels: 48.5 us -> 44.1 us
    pallas_call x2, Pallas kernels: 48.5 us -> 44.1 us  [the longest x1 42.9 us: per_device(): pl.pallas_call(kernel, out_shape=(jax.ShapeDtypeStruct((2, SIDE, 4, PER_O...]
where the time goes in v4:
time: 45 us; the launch traced here: 44.8 us
  Pallas kernels  44.1 us (98%)
  between operations  0.64 us (1%)
    pallas_call x1, Pallas kernels, per_device(): pl.pallas_call(kernel, out_shape=(jax.ShapeDtypeStruct((2, SIDE, 4, PER_O...  42.9 us
    pallas_call x1, Pallas kernels, per_device(): pl.pallas_call(deliver, out_shape=outs, in_specs=[vmem] * 3, out_specs=(h...  1.21 us

profile of v4, /device:TPU:6, one launch (start us, length us, event | category | flops | bytes accessed | tf_op | source)
XLA Modules:
  0.0 44.8 jit_solution(11057937168732489733)
XLA Ops:
  0.6 42.9 %shard_map.68 = (f32[2,8,4,32,128]{4,3,2,1,0:T(8,128)S(1)}, f32[2048,128]{1,0:T(8,128)S(1)}, bf16[64,256]{1,0:T(8,128)(2,1)S(1)}) custom-call(bf16[1,2,256,2048]{3,2,1,0:T(8,128)(2,1)} %x_hbm.1, bf16[1,2,256,128]{3,2,1,0:T(8,128)(2,1)} %g_hbm.1, f32[1,2048,128]{2,1,0:T(8,128)} %m_hbm.1, s32[64,2,8,64]{3,2,1,0:T(8,128)} %bitcast.2, ...), custom_call_target="tpu_custom_call" | custom-call | tf_op jit(solution)/shard_map/pallas_call | solution.py:383
  43.6 1.2 %shard_map.69 = (bf16[2048,128]{1,0:T(8,128)(2,1)}, f32[2048,128]{1,0:T(8,128)}) custom-call(f32[2,8,4,32,128]{4,3,2,1,0:T(8,128)S(1)} %get-tuple-element.7.u_ref, f32[2048,128]{1,0:T(8,128)S(1)} %get-tuple-element.8.mom_ref, bf16[64,256]{1,0:T(8,128)(2,1)S(1)} %get-tuple-element.9.back_ref), custom_call_target="tpu_custom_call" | custom-call | tf_op jit(solution)/shard_map/pallas_call | solution.py:425

commit v5 on v4

--- a/solution.py
+++ b/solution.py
@@ -33,7 +33,7 @@
     def parts(table):
         high = table.astype(BF16)
         low = (table - high.astype(np.float32)).astype(BF16)
-        return np.concatenate([high, high, low, low], 1)
+        return np.concatenate([high, high, low, np.zeros_like(low)], 1)
 
     return np.concatenate([parts(dct), parts(dct.T)], 0)
 
@@ -52,23 +52,33 @@
     return x[:, :COLS] + x[:, COLS:]
 
 
-def blocks_apply(table, x):
+def pair_products(tables, x):
     high = x.astype(BF16)
     low = (x - high.astype(F32)).astype(BF16)
 
     def stacked(b):
         rows = slice(b * GROUP, (b + 1) * GROUP)
-        return jnp.concatenate([high[rows], low[rows]], axis=0)
-
+        return jnp.concatenate([high[rows], low[rows], high[rows]], axis=0)
+
+    return [
+        dot(tables[p], jnp.concatenate([stacked(2 * p), stacked(2 * p + 1)], axis=1))
+        for p in range(SPAN // GROUP // 2)
+    ]
+
+
+def blocks_of(products):
     out = []
-    for b in range(0, SPAN // GROUP, 2):
-        pair = jnp.concatenate([stacked(b), stacked(b + 1)], axis=1)
-        r = dot(table, jnp.concatenate([pair, pair], axis=0))
-        out += [r[:, :COLS], r[:, COLS:]]
+    for r in products:
+        out += [r[:GROUP, :COLS], r[:GROUP, COLS:]]
     return jnp.concatenate(out, axis=0)
 
 
-CHUNKS = 2
+def blocks_apply(table, x):
+    return blocks_of(pair_products([table[:, :DEPTH]] * 2, x))
+
+
+DEPTH = 3 * GROUP
+CHUNKS = 4
 HALVES = 2
 PER_CHUNK = 4 // CHUNKS
 
@@ -76,7 +86,7 @@
 def kernel(
     x_hbm, g_hbm, m_hbm, sel_hbm, tab_hbm,
     u_v, mom_ref, back_v,
-    x_v, g_v, m_v, sel_v, own_v, tab_v, f_v, kept_v, pick_v, keep_v,
+    x_v, g_v, m_v, sel_v, own_v, tab_v, f_v, kept_v, pick_v, tsel_v, ext_v,
     zsend, ysend, zin, yin, pz, py, p2in, tout,
     load_sem, r1s, r1r, p2s, p2r, a1s, a1r, a2s, a2r,
 ):
@@ -88,6 +98,11 @@
 
     def at(yy, zz):
         return (yy * SIDE + zz, mp)
+
+    barrier = pltpu.get_barrier_semaphore()
+    for d in range(1, SIDE):
+        pl.semaphore_signal(barrier, inc=1, device_id=at((y + d) % SIDE, z), device_id_type=MESH)
+        pl.semaphore_signal(barrier, inc=1, device_id=at(y, (z + d) % SIDE), device_id_type=MESH)
 
     loads = []
 
@@ -114,11 +129,6 @@
     load_sel = load(sel_hbm, sel_v)
     load_back = load(tab_hbm.at[pl.ds(GROUP, GROUP)], back_v)
 
-    barrier = pltpu.get_barrier_semaphore()
-    for d in range(1, SIDE):
-        pl.semaphore_signal(barrier, inc=1, device_id=at((y + d) % SIDE, z), device_id_type=MESH)
-        pl.semaphore_signal(barrier, inc=1, device_id=at(y, (z + d) % SIDE), device_id_type=MESH)
-
     def first(axis, d, c):
         part = pl.ds(c * PER_CHUNK, PER_CHUNK)
         to = ((z if axis == 0 else y) + d) % SIDE
@@ -129,11 +139,31 @@
             device_id=at(y, to) if axis == 0 else at(to, z), device_id_type=MESH,
         )
 
+    def send_half(half):
+        for c in range(CHUNKS):
+            if c * HALVES // CHUNKS == half:
+                for d in FAR_FIRST:
+                    first(0, d, c).start()
+        for c in range(CHUNKS):
+            for g in range(half * SIDE // HALVES, (half + 1) * SIDE // HALVES):
+
+                @pl.when(y != g)
+                def _():
+                    first(1, (g - y + SIDE) % SIDE, c).start()
+
     tn = (((0,), (0,)), ((), ()))
     lane = lax.broadcasted_iota(jnp.int32, (CAP, SPAN), 1)
     ones = jnp.ones((SIDE * CAP, COLS), BF16)
     owner_lane = lax.broadcasted_iota(jnp.int32, (CAP, SIDE * SIDE), 1)
     load_own.wait()
+    load_tab.wait()
+    table = tab_v[...]
+    stack = jnp.concatenate([table] * (SPAN // GROUP), axis=0)
+    second_list = own_v[1]
+    again = second_list == own_v[0, 0:1, :]
+    for j in range(1, CAP):
+        again = jnp.logical_or(again, second_list == own_v[0, j : j + 1, :])
+    fresh = jnp.where(again, 0.0, DECAY).astype(F32)
     for s in range(STEPS):
         own = own_v[s]
         own = jnp.where(own >= 0, own + (owner_lane % SIDE) * PER_OWNER, -1)
@@ -144,9 +174,17 @@
             ]
             onehot = jnp.concatenate(picks, axis=0).astype(BF16)
             pick_v[s, g] = onehot
-            keep_v[s, g] = 1.0 - dot(onehot, ones, tn)
+            tsel_v[s, g] = dot(onehot, stack).astype(BF16)
     load_g.wait()
-    load_tab.wait()
+
+    def rows_of(s, g, p):
+        return tsel_v[s, g, p * 4 * CAP : (p + 1) * 4 * CAP, :DEPTH]
+
+    def tile_of(products, base, q):
+        side = (q // 2) % 2 * COLS
+        top = base + q % 4 * CAP
+        return products[q // 4][top : top + CAP, side : side + COLS]
+
     for half in range(HALVES):
         groups = range(half * SIDE // HALVES, (half + 1) * SIDE // HALVES)
         load_half[half][0].wait()
@@ -160,34 +198,31 @@
             f_v[1, g] = dot(x_v[1, :, rows], g_v[1], tn)
         for s in range(STEPS):
             for g in groups:
-                c = blocks_apply(tab_v[...], f_v[s, g])
-                if s:
-                    c = c + DECAY * kept_v[g]
-                packed = folded(dot(pick_v[s, g], split(c)))
-                kept_v[g] = keep_v[s, g] * c
+                tables = [
+                    jnp.concatenate(
+                        [table[:, :DEPTH]] + [rows_of(t, g, p) for t in range(s, STEPS)],
+                        axis=0,
+                    )
+                    for p in range(2)
+                ]
+                products = pair_products(tables, f_v[s, g])
+                f_v[s, g] = blocks_of(products)
                 for q in range(SIDE):
-                    tile = packed[q * CAP : (q + 1) * CAP]
+                    tile = tile_of(products, GROUP, q)
+                    if s == 0:
+                        o = g * SIDE + q
+                        ext_v[g, q] = fresh[:, o : o + 1] * tile_of(
+                            products, GROUP + 4 * CAP, q
+                        )
+                    else:
+                        tile = tile + ext_v[g, q]
                     if (g + q) % 2 == 0:
                         zsend[q, g // 2, s * CAP : (s + 1) * CAP, :] = tile
                     else:
                         ysend[g, q // 2, s * CAP : (s + 1) * CAP, :] = tile
         if half == 0:
             pl.semaphore_wait(barrier, 2 * (SIDE - 1))
-        for c in range(CHUNKS):
-            if c * HALVES // CHUNKS == half:
-                for d in FAR_FIRST:
-                    first(0, d, c).start()
-        if HALVES == 1:
-            for c in range(CHUNKS):
-                for d in FAR_FIRST:
-                    first(1, d, c).start()
-        else:
-            for c in range(CHUNKS):
-                for g in groups:
-
-                    @pl.when(y != g)
-                    def _():
-                        first(1, (g - y + SIDE) % SIDE, c).start()
+        send_half(half)
 
     zin[z] = zsend[z]
     yin[y] = ysend[y]
@@ -213,6 +248,9 @@
     table_y = scatter_table(along_y, y * SIDE + 2 * index + (y + 1) % 2)
 
     backward = back_v[...]
+    for g in range(SIDE):
+        keep = [1.0 - dot(pick_v[s, g], ones, tn) for s in range(STEPS)]
+        kept_v[g] = keep[1] * (DECAY * keep[0] * f_v[0, g] + f_v[1, g])
     for g in range(SIDE):
         mom_ref[g * SPAN : (g + 1) * SPAN, :] = blocks_apply(backward, kept_v[g])
 
@@ -399,7 +437,8 @@
             pltpu.VMEM((STEPS, SIDE, SPAN, COLS), F32),
             pltpu.VMEM((SIDE, SPAN, COLS), F32),
             pltpu.VMEM((STEPS, SIDE, SIDE * CAP, SPAN), BF16),
-            pltpu.VMEM((STEPS, SIDE, SPAN, COLS), F32),
+            pltpu.VMEM((STEPS, SIDE, SIDE * CAP, SPAN), BF16),
+            pltpu.VMEM((SIDE, SIDE, CAP, COLS), F32),
             pltpu.VMEM((SIDE, 4, STEPS * CAP, COLS), F32),
             pltpu.VMEM((SIDE, 4, STEPS * CAP, COLS), F32),
             pltpu.VMEM((SIDE, 4, STEPS * CAP, COLS), F32),

time: 45 us -> 43.5 us (0.967)
  Pallas kernels: 44.1 us -> 42.7 us
    pallas_call x1, Pallas kernels: 42.9 us -> 41.5 us  [per_device(): pl.pallas_call(kernel, out_shape=(jax.ShapeDtypeStruct((2, SIDE, 4, PER_O...]
where the time goes in v5:
time: 43.5 us; the launch traced here: 43.3 us
  Pallas kernels  42.7 us (98%)
  between operations  0.64 us (1%)
    pallas_call x1, Pallas kernels, per_device(): pl.pallas_call(kernel, out_shape=(jax.ShapeDtypeStruct((2, SIDE, 4, PER_O...  41.5 us
    pallas_call x1, Pallas kernels, per_device(): pl.pallas_call(deliver, out_shape=outs, in_specs=[vmem] * 3, out_specs=(h...  1.21 us

profile of v5, /device:TPU:6, one launch (start us, length us, event | category | flops | bytes accessed | tf_op | source)
XLA Modules:
  0.0 43.3 jit_solution(5321002030892914562)
XLA Ops:
  0.6 41.5 %shard_map.68 = (f32[2,8,4,32,128]{4,3,2,1,0:T(8,128)S(1)}, f32[2048,128]{1,0:T(8,128)S(1)}, bf16[64,256]{1,0:T(8,128)(2,1)S(1)}) custom-call(bf16[1,2,256,2048]{3,2,1,0:T(8,128)(2,1)} %x_hbm.1, bf16[1,2,256,128]{3,2,1,0:T(8,128)(2,1)} %g_hbm.1, f32[1,2048,128]{2,1,0:T(8,128)} %m_hbm.1, s32[64,2,8,64]{3,2,1,0:T(8,128)} %bitcast.2, ...), custom_call_target="tpu_custom_call" | custom-call | tf_op jit(solution)/shard_map/pallas_call | solution.py:421
  42.1 1.2 %shard_map.69 = (bf16[2048,128]{1,0:T(8,128)(2,1)}, f32[2048,128]{1,0:T(8,128)}) custom-call(f32[2,8,4,32,128]{4,3,2,1,0:T(8,128)S(1)} %get-tuple-element.7.u_ref, f32[2048,128]{1,0:T(8,128)S(1)} %get-tuple-element.8.mom_ref, bf16[64,256]{1,0:T(8,128)(2,1)S(1)} %get-tuple-element.9.back_ref), custom_call_target="tpu_custom_call" | custom-call | tf_op jit(solution)/shard_map/pallas_call | solution.py:464

commit v6 on v5

--- a/solution.py
+++ b/solution.py
@@ -359,8 +359,8 @@
         for axis in range(2):
             for i in (2 * half, 2 * half + 1):
                 third_arrived(axis, i)
-            for way in range(2):
-                spread(axis, way, 2, 0, 2 * half, 2).start()
+                for way in range(2):
+                    spread(axis, way, 2, 0, i, 1).start()
     for axis in range(2):
         for way in range(2):
             spread(axis, way, 1, 0, 0, 4).start()

time: 43.5 us -> 43.3 us (level)
  no operation moved by 1% of the time
where the time goes in v6:
time: 43.3 us; the launch traced here: 43.1 us
  Pallas kernels  42.5 us (98%)
  between operations  0.64 us (1%)
    pallas_call x1, Pallas kernels, per_device(): pl.pallas_call(kernel, out_shape=(jax.ShapeDtypeStruct((2, SIDE, 4, PER_O...  41.3 us
    pallas_call x1, Pallas kernels, per_device(): pl.pallas_call(deliver, out_shape=outs, in_specs=[vmem] * 3, out_specs=(h...  1.21 us

profile of v6, /device:TPU:6, one launch (start us, length us, event | category | flops | bytes accessed | tf_op | source)
XLA Modules:
  0.0 43.1 jit_solution(9963490549358201072)
XLA Ops:
  0.6 41.3 %shard_map.68 = (f32[2,8,4,32,128]{4,3,2,1,0:T(8,128)S(1)}, f32[2048,128]{1,0:T(8,128)S(1)}, bf16[64,256]{1,0:T(8,128)(2,1)S(1)}) custom-call(bf16[1,2,256,2048]{3,2,1,0:T(8,128)(2,1)} %x_hbm.1, bf16[1,2,256,128]{3,2,1,0:T(8,128)(2,1)} %g_hbm.1, f32[1,2048,128]{2,1,0:T(8,128)} %m_hbm.1, s32[64,2,8,64]{3,2,1,0:T(8,128)} %bitcast.2, ...), custom_call_target="tpu_custom_call" | custom-call | tf_op jit(solution)/shard_map/pallas_call | solution.py:421
  41.9 1.2 %shard_map.69 = (bf16[2048,128]{1,0:T(8,128)(2,1)}, f32[2048,128]{1,0:T(8,128)}) custom-call(f32[2,8,4,32,128]{4,3,2,1,0:T(8,128)S(1)} %get-tuple-element.7.u_ref, f32[2048,128]{1,0:T(8,128)S(1)} %get-tuple-element.8.mom_ref, bf16[64,256]{1,0:T(8,128)(2,1)S(1)} %get-tuple-element.9.back_ref), custom_call_target="tpu_custom_call" | custom-call | tf_op jit(solution)/shard_map/pallas_call | solution.py:464

commit v7 on v6

--- a/solution.py
+++ b/solution.py
@@ -356,8 +356,8 @@
         await_recv(block, a2r.at[axis, 2 * (distance - 1) + way, first_block // 2])
 
     for half in range(2):
-        for axis in range(2):
-            for i in (2 * half, 2 * half + 1):
+        for i in (2 * half, 2 * half + 1):
+            for axis in range(2):
                 third_arrived(axis, i)
                 for way in range(2):
                     spread(axis, way, 2, 0, i, 1).start()

time: 43.3 us -> 43.4 us (level)
  no operation moved by 1% of the time
where the time goes in v7:
time: 43.4 us; the launch traced here: 43 us
  Pallas kernels  42.4 us (98%)
  between operations  0.64 us (1%)
    pallas_call x1, Pallas kernels, per_device(): pl.pallas_call(kernel, out_shape=(jax.ShapeDtypeStruct((2, SIDE, 4, PER_O...  41.1 us
    pallas_call x1, Pallas kernels, per_device(): pl.pallas_call(deliver, out_shape=outs, in_specs=[vmem] * 3, out_specs=(h...  1.21 us

profile of v7, /device:TPU:6, one launch (start us, length us, event | category | flops | bytes accessed | tf_op | source)
XLA Modules:
  0.0 43.0 jit_solution(13978468262189105804)
XLA Ops:
  0.6 41.1 %shard_map.68 = (f32[2,8,4,32,128]{4,3,2,1,0:T(8,128)S(1)}, f32[2048,128]{1,0:T(8,128)S(1)}, bf16[64,256]{1,0:T(8,128)(2,1)S(1)}) custom-call(bf16[1,2,256,2048]{3,2,1,0:T(8,128)(2,1)} %x_hbm.1, bf16[1,2,256,128]{3,2,1,0:T(8,128)(2,1)} %g_hbm.1, f32[1,2048,128]{2,1,0:T(8,128)} %m_hbm.1, s32[64,2,8,64]{3,2,1,0:T(8,128)} %bitcast.2, ...), custom_call_target="tpu_custom_call" | custom-call | tf_op jit(solution)/shard_map/pallas_call | solution.py:421
  41.8 1.2 %shard_map.69 = (bf16[2048,128]{1,0:T(8,128)(2,1)}, f32[2048,128]{1,0:T(8,128)}) custom-call(f32[2,8,4,32,128]{4,3,2,1,0:T(8,128)S(1)} %get-tuple-element.7.u_ref, f32[2048,128]{1,0:T(8,128)S(1)} %get-tuple-element.8.mom_ref, bf16[64,256]{1,0:T(8,128)(2,1)S(1)} %get-tuple-element.9.back_ref), custom_call_target="tpu_custom_call" | custom-call | tf_op jit(solution)/shard_map/pallas_call | solution.py:464
